TPU v7x, 16 devices: a 4x2x1 block of a 4x4x8 slice. The times are simulated.
16 devices in a mesh: dp: 2 (over y, z), fsdp: 8 (over x, core).
Axes of the slice: x: 4, y: 2, z: 1, core: 2. Of those that a mesh axis runs over, the one named last changes fastest.
The devices are a block of a 4x4x8 slice.
Arguments:
- hidden: bfloat16 [2, 32768, 512], P(None, ('dp', 'fsdp')), parts along dimension 1
- targets: int32 [2, 32768], P(None, ('dp', 'fsdp')), parts along dimension 1
- w_out: bfloat16 [32128, 512], P('fsdp')
Outputs:
- output 1: float32 [4], P('dp'), parts along dimension 0
- output 2: float32 [2, 32768, 512], P(None, ('dp', 'fsdp')), parts along dimension 1
- output 3: float32 [64256, 512], P(('dp', 'fsdp')), parts along dimension 0
There are 2 independent parts. A program takes and returns all parts, laid end to end along the dimension named above; an argument that names none is the same for every part.
All inputs are finite; a program needn't handle non-finite values.
Results may differ from a plain program's by a relative error of at most 0.001.
Values are sent between devices in bfloat16 or wider.
A program may use at most 768 MiB of HBM per device.

v0:
```python
import jax
import jax.numpy as jnp
from jax import lax
from jax.sharding import PartitionSpec as P


def solution(mesh):
    group_size = mesh.shape['fsdp']
    shift_perm = [(src_idx, (src_idx - 1) % group_size) for src_idx in range(group_size)]

    def local_head(hidden, targets, w_loc):
        n_micro, tok_dev, model_dim = hidden.shape
        blk_rows = w_loc.shape[0]
        tokens = tok_dev * group_size
        n_rows = n_micro * tok_dev
        tok_rows = hidden.reshape(n_rows, model_dim)
        row_tgt = targets.reshape(n_rows)
        col_ids = lax.broadcasted_iota(jnp.int32, (1, blk_rows), 1)
        my_idx = lax.axis_index('fsdp')

        def block_logits(w_blk, step_idx):
            blk_idx = (my_idx + step_idx) % group_size
            logits = lax.dot_general(tok_rows, w_blk, (((1,), (1,)), ((), ())), preferred_element_type=jnp.float32)
            tgt_hit = (row_tgt - blk_idx * blk_rows)[:, None] == col_ids
            return logits, tgt_hit

        def fwd_update(run_stats, w_blk, step_idx):
            run_max, run_sum, tgt_logit = run_stats
            logits, tgt_hit = block_logits(w_blk, step_idx)
            tgt_logit = tgt_logit + jnp.sum(jnp.where(tgt_hit, logits, 0.0), axis=1)
            new_max = jnp.maximum(run_max, jnp.max(logits, axis=1))
            run_sum = run_sum * jnp.exp(run_max - new_max) + jnp.sum(jnp.exp(logits - new_max[:, None]), axis=1)
            return new_max, run_sum, tgt_logit

        init_stats = (jnp.full((n_rows,), -jnp.inf, jnp.float32), jnp.zeros((n_rows,), jnp.float32), jnp.zeros((n_rows,), jnp.float32))
        first_stats = fwd_update(init_stats, w_loc, 0)

        def fwd_body(step_idx, loop_carry):
            w_cur, run_stats = loop_carry
            w_cur = lax.ppermute(w_cur, 'fsdp', shift_perm)
            return w_cur, fwd_update(run_stats, w_cur, step_idx)

        _, (run_max, run_sum, tgt_logit) = lax.fori_loop(1, group_size, fwd_body, (w_loc, first_stats))
        log_norm = run_max + jnp.log(run_sum)
        loss_vals = lax.psum(jnp.sum((log_norm - tgt_logit).reshape(n_micro, tok_dev), axis=1) / tokens, 'fsdp')

        def bwd_update(d_rows, w_blk, step_idx):
            logits, tgt_hit = block_logits(w_blk, step_idx)
            soft_probs = jnp.exp(logits - log_norm[:, None])
            d_logits = ((soft_probs - tgt_hit.astype(jnp.float32)) / tokens).astype(jnp.bfloat16)
            d_rows = d_rows + jnp.dot(d_logits, w_blk, preferred_element_type=jnp.float32)
            d_w_part = lax.dot_general(d_logits, tok_rows, (((0,), (0,)), ((), ())), preferred_element_type=jnp.float32)
            return d_rows, d_w_part

        d_rows, d_w_acc = bwd_update(jnp.zeros((n_rows, model_dim), jnp.float32), w_loc, 0)

        def bwd_body(step_idx, loop_carry):
            w_cur, d_w_acc, d_rows = loop_carry
            w_cur = lax.ppermute(w_cur, 'fsdp', shift_perm)
            d_w_acc = lax.ppermute(d_w_acc, 'fsdp', shift_perm)
            d_rows, d_w_part = bwd_update(d_rows, w_cur, step_idx)
            return w_cur, d_w_acc + d_w_part, d_rows

        _, d_w_acc, d_rows = lax.fori_loop(1, group_size, bwd_body, (w_loc, d_w_acc, d_rows))
        d_w = lax.ppermute(d_w_acc, 'fsdp', shift_perm)
        return loss_vals, d_rows.reshape(n_micro, tok_dev, model_dim), d_w

    return jax.shard_map(local_head, mesh=mesh,
                         in_specs=(P(None, ('dp', 'fsdp'), None), P(None, ('dp', 'fsdp')), P('fsdp', None)),
                         out_specs=(P('dp'), P(None, ('dp', 'fsdp'), None), P(('dp', 'fsdp'), None)),
                         check_vma=False)
```

profile of v0, /device:TPU:113, one launch (start us, length us, event | category | flops | bytes accessed | tf_op | source)
XLA Modules:
  0.0 2100.3 jit_solution(11395992497151641124)
XLA Ops:
  10.1 29.6 %fusion.8 = (f32[4096]{0:T(1024)S(1)}, f32[4096,4016]{0,1:T(8,128)}) fusion(bf16[4096,512]{1,0:T(8,128)(2,1)} %bitcast.35, bf16[4016,512]{1,0:T(8,128)(2,1)} %copy.36), kind=kOutput, calls=%fused_computation.24 | convolution fusion | flops 16860770304 | bytes 74121216 | tf_op jit(solution)/shard_map/dot_general | solution.py:23
  61.1 717.7 %while.42 = (s32[]{:T(128)}, bf16[4016,512]{1,0:T(8,128)(2,1)}, f32[4096]{0:T(1024)S(1)}, f32[4096]{0:T(1024)S(1)}, f32[4096]{0:T(1024)S(1)}, /*index=5*/bf16[40...) while((s32[]{:T(128)}, bf16[4016,512]{1,0:T(8,128)(2,1)}, ...), condition=%wide.region_7.8_spmd.clone, body=%wide.region_3.7_spmd.clone.sunk | while | flops 16943034368 | bytes 164905264 | solution.py:43
  62.1 47.3 %collective-permute-done = bf16[4016,512]{1,0:T(8,128)(2,1)} collective-permute-done((bf16[4016,512]{1,0:T(8,128)(2,1)}, bf16[4016,512]{1,0:T(8,128)(2,1)}, u32[]{:S(2)}, u32[]{:S(2)}) %collective-permute-start) | collective-permute-done | bytes 4112416 | tf_op jit(solution)/shard_map/while/body/eval_jaxpr/ppermute | solution.py:40
  109.3 29.5 %fusion.32 = (f32[4096]{0:T(1024)S(1)}, f32[4096,4016]{0,1:T(8,128)}) fusion(bf16[4096,512]{1,0:T(8,128)(2,1)} %get-tuple-element.668, bf16[4016,512]{1,0:T(8,128)(2,1)} %collective-permute-done), kind=kOutput, calls=%fused_computation.23.clone.1 | convolution fusion | flops 16860770304 | bytes 74121216 | tf_op jit(solution)/shard_map/while/body/eval_jaxpr/dot_general | solution.py:23
  165.9 45.8 %collective-permute-done = bf16[4016,512]{1,0:T(8,128)(2,1)} collective-permute-done((bf16[4016,512]{1,0:T(8,128)(2,1)}, bf16[4016,512]{1,0:T(8,128)(2,1)}, u32[]{:S(2)}, u32[]{:S(2)}) %collective-permute-start) | collective-permute-done | bytes 4112416 | tf_op jit(solution)/shard_map/while/body/eval_jaxpr/ppermute | solution.py:40
  211.7 29.5 %fusion.32 = (f32[4096]{0:T(1024)S(1)}, f32[4096,4016]{0,1:T(8,128)}) fusion(bf16[4096,512]{1,0:T(8,128)(2,1)} %get-tuple-element.668, bf16[4016,512]{1,0:T(8,128)(2,1)} %collective-permute-done), kind=kOutput, calls=%fused_computation.23.clone.1 | convolution fusion | flops 16860770304 | bytes 74121216 | tf_op jit(solution)/shard_map/while/body/eval_jaxpr/dot_general | solution.py:23
  269.5 44.6 %collective-permute-done = bf16[4016,512]{1,0:T(8,128)(2,1)} collective-permute-done((bf16[4016,512]{1,0:T(8,128)(2,1)}, bf16[4016,512]{1,0:T(8,128)(2,1)}, u32[]{:S(2)}, u32[]{:S(2)}) %collective-permute-start) | collective-permute-done | bytes 4112416 | tf_op jit(solution)/shard_map/while/body/eval_jaxpr/ppermute | solution.py:40
  314.1 29.5 %fusion.32 = (f32[4096]{0:T(1024)S(1)}, f32[4096,4016]{0,1:T(8,128)}) fusion(bf16[4096,512]{1,0:T(8,128)(2,1)} %get-tuple-element.668, bf16[4016,512]{1,0:T(8,128)(2,1)} %collective-permute-done), kind=kOutput, calls=%fused_computation.23.clone.1 | convolution fusion | flops 16860770304 | bytes 74121216 | tf_op jit(solution)/shard_map/while/body/eval_jaxpr/dot_general | solution.py:23
  373.0 43.4 %collective-permute-done = bf16[4016,512]{1,0:T(8,128)(2,1)} collective-permute-done((bf16[4016,512]{1,0:T(8,128)(2,1)}, bf16[4016,512]{1,0:T(8,128)(2,1)}, u32[]{:S(2)}, u32[]{:S(2)}) %collective-permute-start) | collective-permute-done | bytes 4112416 | tf_op jit(solution)/shard_map/while/body/eval_jaxpr/ppermute | solution.py:40
  416.4 29.5 %fusion.32 = (f32[4096]{0:T(1024)S(1)}, f32[4096,4016]{0,1:T(8,128)}) fusion(bf16[4096,512]{1,0:T(8,128)(2,1)} %get-tuple-element.668, bf16[4016,512]{1,0:T(8,128)(2,1)} %collective-permute-done), kind=kOutput, calls=%fused_computation.23.clone.1 | convolution fusion | flops 16860770304 | bytes 74121216 | tf_op jit(solution)/shard_map/while/body/eval_jaxpr/dot_general | solution.py:23
  476.6 42.2 %collective-permute-done = bf16[4016,512]{1,0:T(8,128)(2,1)} collective-permute-done((bf16[4016,512]{1,0:T(8,128)(2,1)}, bf16[4016,512]{1,0:T(8,128)(2,1)}, u32[]{:S(2)}, u32[]{:S(2)}) %collective-permute-start) | collective-permute-done | bytes 4112416 | tf_op jit(solution)/shard_map/while/body/eval_jaxpr/ppermute | solution.py:40
  518.8 29.5 %fusion.32 = (f32[4096]{0:T(1024)S(1)}, f32[4096,4016]{0,1:T(8,128)}) fusion(bf16[4096,512]{1,0:T(8,128)(2,1)} %get-tuple-element.668, bf16[4016,512]{1,0:T(8,128)(2,1)} %collective-permute-done), kind=kOutput, calls=%fused_computation.23.clone.1 | convolution fusion | flops 16860770304 | bytes 74121216 | tf_op jit(solution)/shard_map/while/body/eval_jaxpr/dot_general | solution.py:23
  580.2 41.0 %collective-permute-done = bf16[4016,512]{1,0:T(8,128)(2,1)} collective-permute-done((bf16[4016,512]{1,0:T(8,128)(2,1)}, bf16[4016,512]{1,0:T(8,128)(2,1)}, u32[]{:S(2)}, u32[]{:S(2)}) %collective-permute-start) | collective-permute-done | bytes 4112416 | tf_op jit(solution)/shard_map/while/body/eval_jaxpr/ppermute | solution.py:40
  621.1 29.5 %fusion.32 = (f32[4096]{0:T(1024)S(1)}, f32[4096,4016]{0,1:T(8,128)}) fusion(bf16[4096,512]{1,0:T(8,128)(2,1)} %get-tuple-element.668, bf16[4016,512]{1,0:T(8,128)(2,1)} %collective-permute-done), kind=kOutput, calls=%fused_computation.23.clone.1 | convolution fusion | flops 16860770304 | bytes 74121216 | tf_op jit(solution)/shard_map/while/body/eval_jaxpr/dot_general | solution.py:23
  683.8 39.8 %collective-permute-done = bf16[4016,512]{1,0:T(8,128)(2,1)} collective-permute-done((bf16[4016,512]{1,0:T(8,128)(2,1)}, bf16[4016,512]{1,0:T(8,128)(2,1)}, u32[]{:S(2)}, u32[]{:S(2)}) %collective-permute-start) | collective-permute-done | bytes 4112416 | tf_op jit(solution)/shard_map/while/body/eval_jaxpr/ppermute | solution.py:40
  723.5 29.5 %fusion.32 = (f32[4096]{0:T(1024)S(1)}, f32[4096,4016]{0,1:T(8,128)}) fusion(bf16[4096,512]{1,0:T(8,128)(2,1)} %get-tuple-element.668, bf16[4016,512]{1,0:T(8,128)(2,1)} %collective-permute-done), kind=kOutput, calls=%fused_computation.23.clone.1 | convolution fusion | flops 16860770304 | bytes 74121216 | tf_op jit(solution)/shard_map/while/body/eval_jaxpr/dot_general | solution.py:23
  779.4 29.5 %fusion.4 = f32[4096,512]{1,0:T(8,128)} fusion(bf16[4016,512]{1,0:T(8,128)(2,1)} %copy.36, f32[4096,4016]{0,1:T(8,128)} %get-tuple-element.530, f32[4096]{0:T(1024)S(1)} %get-tuple-element.681, s32[4096]{0:T(1024)S(1)} %copy-done.1), kind=kOutput, calls=%fused_computation.20 | convolution fusion | flops 16943022080 | bytes 78331904 | tf_op jit(solution)/shard_map/dot_general | solution.py:51
  808.9 29.4 %fusion.5 = f32[4016,512]{1,0:T(8,128)} fusion(bf16[4096,512]{1,0:T(8,128)(2,1)} %get-tuple-element.726, f32[4096,4016]{0,1:T(8,128)} %get-tuple-element.530, f32[4096]{0:T(1024)S(1)} %get-tuple-element.681, s32[4096]{0:T(1024)S(1)} %copy-done.1), kind=kOutput, calls=%fused_computation.21 | convolution fusion | flops 16943022080 | bytes 78249984 | tf_op jit(solution)/shard_map/dot_general | solution.py:52
  838.3 1138.4 %while.43 = (s32[]{:T(128)}, bf16[4016,512]{1,0:T(8,128)(2,1)}, f32[4016,512]{1,0:T(8,128)}, f32[4096,512]{1,0:T(8,128)}, bf16[4096,512]{1,0:T(8,128)(2,1)}, /*i...) while((s32[]{:T(128)}, bf16[4016,512]{1,0:T(8,128)(2,1)}, ...), condition=%wide.region_11.12_spmd.clone, body=%wide.region_10.11_spmd.clone.sunk | while | flops 50635829248 | bytes 206176592 | solution.py:64
  864.4 35.4 %collective-permute-done.1 = bf16[4016,512]{1,0:T(8,128)(2,1)} collective-permute-done((bf16[4016,512]{1,0:T(8,128)(2,1)}, bf16[4016,512]{1,0:T(8,128)(2,1)}, u32[]{:S(2)}, u32[]{:S(2)}) %collective-permute-start.1) | collective-permute-done | bytes 4112416 | tf_op jit(solution)/shard_map/while/body/eval_jaxpr/ppermute | solution.py:59
  904.1 30.3 %multiply_convert_fusion.5 = bf16[4096,4016]{0,1:T(8,128)(2,1)} fusion(bf16[4096,512]{1,0:T(8,128)(2,1)} %get-tuple-element.706, bf16[4016,512]{1,0:T(8,128)(2,1)} %collective-permute-done.1, s32[4096]{0:T(1024)S(1)} %broadcast_subtract_fusion.6, f32[4096]{0:T(1024)S(1)} %get-tuple-element.707), kind=kOutput, calls=%fused_computation.8.clone.1 | convolution fusion | flops 16943022080 | bytes 41238528 | tf_op jit(solution)/shard_map/while/body/eval_jaxpr/dot_general | solution.py:23
  1026.2 34.2 %collective-permute-done.1 = bf16[4016,512]{1,0:T(8,128)(2,1)} collective-permute-done((bf16[4016,512]{1,0:T(8,128)(2,1)}, bf16[4016,512]{1,0:T(8,128)(2,1)}, u32[]{:S(2)}, u32[]{:S(2)}) %collective-permute-start.1) | collective-permute-done | bytes 4112416 | tf_op jit(solution)/shard_map/while/body/eval_jaxpr/ppermute | solution.py:59
  1064.7 30.4 %multiply_convert_fusion.5 = bf16[4096,4016]{0,1:T(8,128)(2,1)} fusion(bf16[4096,512]{1,0:T(8,128)(2,1)} %get-tuple-element.706, bf16[4016,512]{1,0:T(8,128)(2,1)} %collective-permute-done.1, s32[4096]{0:T(1024)S(1)} %broadcast_subtract_fusion.6, f32[4096]{0:T(1024)S(1)} %get-tuple-element.707), kind=kOutput, calls=%fused_computation.8.clone.1 | convolution fusion | flops 16943022080 | bytes 41238528 | tf_op jit(solution)/shard_map/while/body/eval_jaxpr/dot_general | solution.py:23
  1187.9 33.0 %collective-permute-done.1 = bf16[4016,512]{1,0:T(8,128)(2,1)} collective-permute-done((bf16[4016,512]{1,0:T(8,128)(2,1)}, bf16[4016,512]{1,0:T(8,128)(2,1)}, u32[]{:S(2)}, u32[]{:S(2)}) %collective-permute-start.1) | collective-permute-done | bytes 4112416 | tf_op jit(solution)/shard_map/while/body/eval_jaxpr/ppermute | solution.py:59
  1225.3 30.4 %multiply_convert_fusion.5 = bf16[4096,4016]{0,1:T(8,128)(2,1)} fusion(bf16[4096,512]{1,0:T(8,128)(2,1)} %get-tuple-element.706, bf16[4016,512]{1,0:T(8,128)(2,1)} %collective-permute-done.1, s32[4096]{0:T(1024)S(1)} %broadcast_subtract_fusion.6, f32[4096]{0:T(1024)S(1)} %get-tuple-element.707), kind=kOutput, calls=%fused_computation.8.clone.1 | convolution fusion | flops 16943022080 | bytes 41238528 | tf_op jit(solution)/shard_map/while/body/eval_jaxpr/dot_general | solution.py:23
  1349.7 31.8 %collective-permute-done.1 = bf16[4016,512]{1,0:T(8,128)(2,1)} collective-permute-done((bf16[4016,512]{1,0:T(8,128)(2,1)}, bf16[4016,512]{1,0:T(8,128)(2,1)}, u32[]{:S(2)}, u32[]{:S(2)}) %collective-permute-start.1) | collective-permute-done | bytes 4112416 | tf_op jit(solution)/shard_map/while/body/eval_jaxpr/ppermute | solution.py:59
  1385.8 30.3 %multiply_convert_fusion.5 = bf16[4096,4016]{0,1:T(8,128)(2,1)} fusion(bf16[4096,512]{1,0:T(8,128)(2,1)} %get-tuple-element.706, bf16[4016,512]{1,0:T(8,128)(2,1)} %collective-permute-done.1, s32[4096]{0:T(1024)S(1)} %broadcast_subtract_fusion.6, f32[4096]{0:T(1024)S(1)} %get-tuple-element.707), kind=kOutput, calls=%fused_computation.8.clone.1 | convolution fusion | flops 16943022080 | bytes 41238528 | tf_op jit(solution)/shard_map/while/body/eval_jaxpr/dot_general | solution.py:23
  1511.5 30.5 %collective-permute-done.1 = bf16[4016,512]{1,0:T(8,128)(2,1)} collective-permute-done((bf16[4016,512]{1,0:T(8,128)(2,1)}, bf16[4016,512]{1,0:T(8,128)(2,1)}, u32[]{:S(2)}, u32[]{:S(2)}) %collective-permute-start.1) | collective-permute-done | bytes 4112416 | tf_op jit(solution)/shard_map/while/body/eval_jaxpr/ppermute | solution.py:59
  1546.4 30.4 %multiply_convert_fusion.5 = bf16[4096,4016]{0,1:T(8,128)(2,1)} fusion(bf16[4096,512]{1,0:T(8,128)(2,1)} %get-tuple-element.706, bf16[4016,512]{1,0:T(8,128)(2,1)} %collective-permute-done.1, s32[4096]{0:T(1024)S(1)} %broadcast_subtract_fusion.6, f32[4096]{0:T(1024)S(1)} %get-tuple-element.707), kind=kOutput, calls=%fused_computation.8.clone.1 | convolution fusion | flops 16943022080 | bytes 41238528 | tf_op jit(solution)/shard_map/while/body/eval_jaxpr/dot_general | solution.py:23
  1707.0 30.3 %multiply_convert_fusion.5 = bf16[4096,4016]{0,1:T(8,128)(2,1)} fusion(bf16[4096,512]{1,0:T(8,128)(2,1)} %get-tuple-element.706, bf16[4016,512]{1,0:T(8,128)(2,1)} %collective-permute-done.1, s32[4096]{0:T(1024)S(1)} %broadcast_subtract_fusion.6, f32[4096]{0:T(1024)S(1)} %get-tuple-element.707), kind=kOutput, calls=%fused_computation.8.clone.1 | convolution fusion | flops 16943022080 | bytes 41238528 | tf_op jit(solution)/shard_map/while/body/eval_jaxpr/dot_general | solution.py:23
  1867.6 30.4 %multiply_convert_fusion.5 = bf16[4096,4016]{0,1:T(8,128)(2,1)} fusion(bf16[4096,512]{1,0:T(8,128)(2,1)} %get-tuple-element.706, bf16[4016,512]{1,0:T(8,128)(2,1)} %collective-permute-done.1, s32[4096]{0:T(1024)S(1)} %broadcast_subtract_fusion.6, f32[4096]{0:T(1024)S(1)} %get-tuple-element.707), kind=kOutput, calls=%fused_computation.8.clone.1 | convolution fusion | flops 16943022080 | bytes 41238528 | tf_op jit(solution)/shard_map/while/body/eval_jaxpr/dot_general | solution.py:23
  1993.9 98.6 %psum.7 = f32[2]{0:T(128)} all-reduce(f32[2]{0:T(128)S(1)} %broadcast_multiply_fusion), channel_id=1, replica_groups=mesh['dp'=2,'fsdp'=8] {'fsdp'}, use_global_device_ids=true, to_apply=%region_9.10 | all-reduce | flops 2 | bytes 16 | tf_op jit(solution)/shard_map/psum | solution.py:45
  (126 shorter events, 1009.7 us)
Async XLA Ops:
  39.7 21.4 %copy-start = (s32[4096]{0:T(1024)}, s32[4096]{0:T(1024)S(1)}, u32[]{:S(2)}) copy-start(s32[4096]{0:T(1024)S(1)} %broadcast_subtract_fusion.2) | copy-start | bytes 49156
  61.1 718.4 %copy-start.1 = (s32[4096]{0:T(1024)S(1)}, s32[4096]{0:T(1024)}, u32[]{:S(2)}) copy-start(s32[4096]{0:T(1024)} %copy-done) | copy-start | bytes 49156
  61.3 48.0 %collective-permute-start = (bf16[4016,512]{1,0:T(8,128)(2,1)}, bf16[4016,512]{1,0:T(8,128)(2,1)}, u32[]{:S(2)}, u32[]{:S(2)}) collective-permute-start(bf16[4016,512]{1,0:T(8,128)(2,1)} %get-tuple-element.651), channel_id=1, source_target_pairs={{0,7},{1,0},{2,1},{3,2},{4,3},{5,4},{6,5},{7,6},{8,15},{9,8},{10,9... | collective-permute-start | bytes 12337160 | tf_op jit(solution)/shard_map/while/body/eval_jaxpr/ppermute | solution.py:40
  164.6 47.1 %collective-permute-start = (bf16[4016,512]{1,0:T(8,128)(2,1)}, bf16[4016,512]{1,0:T(8,128)(2,1)}, u32[]{:S(2)}, u32[]{:S(2)}) collective-permute-start(bf16[4016,512]{1,0:T(8,128)(2,1)} %get-tuple-element.651), channel_id=1, source_target_pairs={{0,7},{1,0},{2,1},{3,2},{4,3},{5,4},{6,5},{7,6},{8,15},{9,8},{10,9... | collective-permute-start | bytes 12337160 | tf_op jit(solution)/shard_map/while/body/eval_jaxpr/ppermute | solution.py:40
  267.0 47.1 %collective-permute-start = (bf16[4016,512]{1,0:T(8,128)(2,1)}, bf16[4016,512]{1,0:T(8,128)(2,1)}, u32[]{:S(2)}, u32[]{:S(2)}) collective-permute-start(bf16[4016,512]{1,0:T(8,128)(2,1)} %get-tuple-element.651), channel_id=1, source_target_pairs={{0,7},{1,0},{2,1},{3,2},{4,3},{5,4},{6,5},{7,6},{8,15},{9,8},{10,9... | collective-permute-start | bytes 12337160 | tf_op jit(solution)/shard_map/while/body/eval_jaxpr/ppermute | solution.py:40
  369.4 47.1 %collective-permute-start = (bf16[4016,512]{1,0:T(8,128)(2,1)}, bf16[4016,512]{1,0:T(8,128)(2,1)}, u32[]{:S(2)}, u32[]{:S(2)}) collective-permute-start(bf16[4016,512]{1,0:T(8,128)(2,1)} %get-tuple-element.651), channel_id=1, source_target_pairs={{0,7},{1,0},{2,1},{3,2},{4,3},{5,4},{6,5},{7,6},{8,15},{9,8},{10,9... | collective-permute-start | bytes 12337160 | tf_op jit(solution)/shard_map/while/body/eval_jaxpr/ppermute | solution.py:40
  471.7 47.1 %collective-permute-start = (bf16[4016,512]{1,0:T(8,128)(2,1)}, bf16[4016,512]{1,0:T(8,128)(2,1)}, u32[]{:S(2)}, u32[]{:S(2)}) collective-permute-start(bf16[4016,512]{1,0:T(8,128)(2,1)} %get-tuple-element.651), channel_id=1, source_target_pairs={{0,7},{1,0},{2,1},{3,2},{4,3},{5,4},{6,5},{7,6},{8,15},{9,8},{10,9... | collective-permute-start | bytes 12337160 | tf_op jit(solution)/shard_map/while/body/eval_jaxpr/ppermute | solution.py:40
  574.1 47.1 %collective-permute-start = (bf16[4016,512]{1,0:T(8,128)(2,1)}, bf16[4016,512]{1,0:T(8,128)(2,1)}, u32[]{:S(2)}, u32[]{:S(2)}) collective-permute-start(bf16[4016,512]{1,0:T(8,128)(2,1)} %get-tuple-element.651), channel_id=1, source_target_pairs={{0,7},{1,0},{2,1},{3,2},{4,3},{5,4},{6,5},{7,6},{8,15},{9,8},{10,9... | collective-permute-start | bytes 12337160 | tf_op jit(solution)/shard_map/while/body/eval_jaxpr/ppermute | solution.py:40
  676.5 47.1 %collective-permute-start = (bf16[4016,512]{1,0:T(8,128)(2,1)}, bf16[4016,512]{1,0:T(8,128)(2,1)}, u32[]{:S(2)}, u32[]{:S(2)}) collective-permute-start(bf16[4016,512]{1,0:T(8,128)(2,1)} %get-tuple-element.651), channel_id=1, source_target_pairs={{0,7},{1,0},{2,1},{3,2},{4,3},{5,4},{6,5},{7,6},{8,15},{9,8},{10,9... | collective-permute-start | bytes 12337160 | tf_op jit(solution)/shard_map/while/body/eval_jaxpr/ppermute | solution.py:40
  838.3 1155.4 %copy-start.2 = (f32[4096]{0:T(1024)S(1)}, f32[4096]{0:T(1024)}, u32[]{:S(2)}) copy-start(f32[4096]{0:T(1024)} %get-tuple-element.525) | copy-start | bytes 49156
  852.7 47.1 %collective-permute-start.1 = (bf16[4016,512]{1,0:T(8,128)(2,1)}, bf16[4016,512]{1,0:T(8,128)(2,1)}, u32[]{:S(2)}, u32[]{:S(2)}) collective-permute-start(bf16[4016,512]{1,0:T(8,128)(2,1)} %get-tuple-element.690), channel_id=1, source_target_pairs={{0,7},{1,0},{2,1},{3,2},{4,3},{5,4},{6,5},{7,6},{8,15},{9,8},{10,9... | collective-permute-start | bytes 12337160 | tf_op jit(solution)/shard_map/while/body/eval_jaxpr/ppermute | solution.py:59
  861.2 126.7 %collective-permute-start.2 = (f32[4016,512]{1,0:T(8,128)}, f32[4016,512]{1,0:T(8,128)}, u32[]{:S(2)}, u32[]{:S(2)}) collective-permute-start(f32[4016,512]{1,0:T(8,128)} %get-tuple-element.691), channel_id=1, source_target_pairs={{0,7},{1,0},{2,1},{3,2},{4,3},{5,4},{6,5},{7,6},{8,15},{9,8},{10,9... | collective-permute-start | bytes 24674312 | tf_op jit(solution)/shard_map/while/body/eval_jaxpr/ppermute | solution.py:60
  1013.3 47.1 %collective-permute-start.1 = (bf16[4016,512]{1,0:T(8,128)(2,1)}, bf16[4016,512]{1,0:T(8,128)(2,1)}, u32[]{:S(2)}, u32[]{:S(2)}) collective-permute-start(bf16[4016,512]{1,0:T(8,128)(2,1)} %get-tuple-element.690), channel_id=1, source_target_pairs={{0,7},{1,0},{2,1},{3,2},{4,3},{5,4},{6,5},{7,6},{8,15},{9,8},{10,9... | collective-permute-start | bytes 12337160 | tf_op jit(solution)/shard_map/while/body/eval_jaxpr/ppermute | solution.py:59
  1023.0 125.5 %collective-permute-start.2 = (f32[4016,512]{1,0:T(8,128)}, f32[4016,512]{1,0:T(8,128)}, u32[]{:S(2)}, u32[]{:S(2)}) collective-permute-start(f32[4016,512]{1,0:T(8,128)} %get-tuple-element.691), channel_id=1, source_target_pairs={{0,7},{1,0},{2,1},{3,2},{4,3},{5,4},{6,5},{7,6},{8,15},{9,8},{10,9... | collective-permute-start | bytes 24674312 | tf_op jit(solution)/shard_map/while/body/eval_jaxpr/ppermute | solution.py:60
  1173.9 47.1 %collective-permute-start.1 = (bf16[4016,512]{1,0:T(8,128)(2,1)}, bf16[4016,512]{1,0:T(8,128)(2,1)}, u32[]{:S(2)}, u32[]{:S(2)}) collective-permute-start(bf16[4016,512]{1,0:T(8,128)(2,1)} %get-tuple-element.690), channel_id=1, source_target_pairs={{0,7},{1,0},{2,1},{3,2},{4,3},{5,4},{6,5},{7,6},{8,15},{9,8},{10,9... | collective-permute-start | bytes 12337160 | tf_op jit(solution)/shard_map/while/body/eval_jaxpr/ppermute | solution.py:59
  1184.8 124.2 %collective-permute-start.2 = (f32[4016,512]{1,0:T(8,128)}, f32[4016,512]{1,0:T(8,128)}, u32[]{:S(2)}, u32[]{:S(2)}) collective-permute-start(f32[4016,512]{1,0:T(8,128)} %get-tuple-element.691), channel_id=1, source_target_pairs={{0,7},{1,0},{2,1},{3,2},{4,3},{5,4},{6,5},{7,6},{8,15},{9,8},{10,9... | collective-permute-start | bytes 24674312 | tf_op jit(solution)/shard_map/while/body/eval_jaxpr/ppermute | solution.py:60
  1334.4 47.1 %collective-permute-start.1 = (bf16[4016,512]{1,0:T(8,128)(2,1)}, bf16[4016,512]{1,0:T(8,128)(2,1)}, u32[]{:S(2)}, u32[]{:S(2)}) collective-permute-start(bf16[4016,512]{1,0:T(8,128)(2,1)} %get-tuple-element.690), channel_id=1, source_target_pairs={{0,7},{1,0},{2,1},{3,2},{4,3},{5,4},{6,5},{7,6},{8,15},{9,8},{10,9... | collective-permute-start | bytes 12337160 | tf_op jit(solution)/shard_map/while/body/eval_jaxpr/ppermute | solution.py:59
  1346.6 123.0 %collective-permute-start.2 = (f32[4016,512]{1,0:T(8,128)}, f32[4016,512]{1,0:T(8,128)}, u32[]{:S(2)}, u32[]{:S(2)}) collective-permute-start(f32[4016,512]{1,0:T(8,128)} %get-tuple-element.691), channel_id=1, source_target_pairs={{0,7},{1,0},{2,1},{3,2},{4,3},{5,4},{6,5},{7,6},{8,15},{9,8},{10,9... | collective-permute-start | bytes 24674312 | tf_op jit(solution)/shard_map/while/body/eval_jaxpr/ppermute | solution.py:60
  1495.0 47.1 %collective-permute-start.1 = (bf16[4016,512]{1,0:T(8,128)(2,1)}, bf16[4016,512]{1,0:T(8,128)(2,1)}, u32[]{:S(2)}, u32[]{:S(2)}) collective-permute-start(bf16[4016,512]{1,0:T(8,128)(2,1)} %get-tuple-element.690), channel_id=1, source_target_pairs={{0,7},{1,0},{2,1},{3,2},{4,3},{5,4},{6,5},{7,6},{8,15},{9,8},{10,9... | collective-permute-start | bytes 12337160 | tf_op jit(solution)/shard_map/while/body/eval_jaxpr/ppermute | solution.py:59
  1508.4 121.8 %collective-permute-start.2 = (f32[4016,512]{1,0:T(8,128)}, f32[4016,512]{1,0:T(8,128)}, u32[]{:S(2)}, u32[]{:S(2)}) collective-permute-start(f32[4016,512]{1,0:T(8,128)} %get-tuple-element.691), channel_id=1, source_target_pairs={{0,7},{1,0},{2,1},{3,2},{4,3},{5,4},{6,5},{7,6},{8,15},{9,8},{10,9... | collective-permute-start | bytes 24674312 | tf_op jit(solution)/shard_map/while/body/eval_jaxpr/ppermute | solution.py:60
  1655.6 47.1 %collective-permute-start.1 = (bf16[4016,512]{1,0:T(8,128)(2,1)}, bf16[4016,512]{1,0:T(8,128)(2,1)}, u32[]{:S(2)}, u32[]{:S(2)}) collective-permute-start(bf16[4016,512]{1,0:T(8,128)(2,1)} %get-tuple-element.690), channel_id=1, source_target_pairs={{0,7},{1,0},{2,1},{3,2},{4,3},{5,4},{6,5},{7,6},{8,15},{9,8},{10,9... | collective-permute-start | bytes 12337160 | tf_op jit(solution)/shard_map/while/body/eval_jaxpr/ppermute | solution.py:59
  1670.1 120.6 %collective-permute-start.2 = (f32[4016,512]{1,0:T(8,128)}, f32[4016,512]{1,0:T(8,128)}, u32[]{:S(2)}, u32[]{:S(2)}) collective-permute-start(f32[4016,512]{1,0:T(8,128)} %get-tuple-element.691), channel_id=1, source_target_pairs={{0,7},{1,0},{2,1},{3,2},{4,3},{5,4},{6,5},{7,6},{8,15},{9,8},{10,9... | collective-permute-start | bytes 24674312 | tf_op jit(solution)/shard_map/while/body/eval_jaxpr/ppermute | solution.py:60
  1816.1 47.1 %collective-permute-start.1 = (bf16[4016,512]{1,0:T(8,128)(2,1)}, bf16[4016,512]{1,0:T(8,128)(2,1)}, u32[]{:S(2)}, u32[]{:S(2)}) collective-permute-start(bf16[4016,512]{1,0:T(8,128)(2,1)} %get-tuple-element.690), channel_id=1, source_target_pairs={{0,7},{1,0},{2,1},{3,2},{4,3},{5,4},{6,5},{7,6},{8,15},{9,8},{10,9... | collective-permute-start | bytes 12337160 | tf_op jit(solution)/shard_map/while/body/eval_jaxpr/ppermute | solution.py:59
  1831.9 119.4 %collective-permute-start.2 = (f32[4016,512]{1,0:T(8,128)}, f32[4016,512]{1,0:T(8,128)}, u32[]{:S(2)}, u32[]{:S(2)}) collective-permute-start(f32[4016,512]{1,0:T(8,128)} %get-tuple-element.691), channel_id=1, source_target_pairs={{0,7},{1,0},{2,1},{3,2},{4,3},{5,4},{6,5},{7,6},{8,15},{9,8},{10,9... | collective-permute-start | bytes 24674312 | tf_op jit(solution)/shard_map/while/body/eval_jaxpr/ppermute | solution.py:60
  1976.7 115.8 %collective-permute-start.3 = (f32[4016,512]{1,0:T(8,128)}, f32[4016,512]{1,0:T(8,128)}, u32[]{:S(2)}, u32[]{:S(2)}) collective-permute-start(f32[4016,512]{1,0:T(8,128)} %get-tuple-element.452), channel_id=1, source_target_pairs={{0,7},{1,0},{2,1},{3,2},{4,3},{5,4},{6,5},{7,6},{8,15},{9,8},{10,9... | collective-permute-start | bytes 24674312 | tf_op jit(solution)/shard_map/ppermute | solution.py:65
where the time goes:
time: 2110 us; the launch traced here: 2100 us
  matrix products  881 us (42%)
  waiting for transfers between devices  705 us (33%)
  other arithmetic  172 us (8%)
  starting transfers between devices  150 us (7%)
  blocking collectives  98.6 us (5%)
  local copies, waits for them, and re-layouts  78.6 us (4%)
    dot_general x15, matrix products, block_logits(): lax.dot_general(tok_rows, w_blk, (((1,), (1,)), ((), ())), preferred_elem...  449 us
    ppermute x7, waiting for transfers between devices, fwd_body(): w_cur = lax.ppermute(w_cur, 'fsdp', shift_perm)  304 us
    dot_general x8, matrix products, bwd_update(): jnp.dot(d_logits, w_blk, preferred_element_type=jnp.float32)  225 us
    ppermute x7, waiting for transfers between devices, bwd_body(): w_cur = lax.ppermute(w_cur, 'fsdp', shift_perm)  222 us
    dot_general x8, matrix products, bwd_update(): lax.dot_general(d_logits, tok_rows, (((0,), (0,)), ((), ())), preferred_e...  207 us
    ppermute x7, waiting for transfers between devices, bwd_body(): d_w_acc = lax.ppermute(d_w_acc, 'fsdp', shift_perm)  178 us
    reduce_sum x8, other arithmetic, fwd_update(): tgt_logit = tgt_logit + jnp.sum(jnp.where(tgt_hit, logits, 0.0), axis=1)  171 us
    psum x1, blocking collectives, local_head(): lax.psum(jnp.sum((log_norm - tgt_logit).reshape(n_micro, tok_dev), axis=1...  98.6 us
  transfers between devices with their start and end apart: 22, of which 21 were waited for; matrix products, arithmetic and copies ran while one was open for 21% of the time, Pallas kernels for 0%

commit v1 on v0

v1 whole, which is shorter than its diff:
```python
import functools

import jax
import jax.numpy as jnp
from jax import lax
from jax.experimental import pallas as pl
from jax.experimental.pallas import tpu as pltpu
from jax.sharding import PartitionSpec as P

F32, BF16, I32 = jnp.float32, jnp.bfloat16, jnp.int32
LOG2E = 1.4426950408889634
LN2 = 0.6931471805599453
BT = 1024
RC = 256
VMEM_LIMIT = 60 << 20
ANY = pl.BlockSpec(memory_space=pl.ANY)
VM = pl.BlockSpec(memory_space=pltpu.VMEM)


def chunks(rows):
    return [(r0, min(RC, rows - r0)) for r0 in range(0, rows, RC)]


def up(a, b):
    return -(-a // b) * b


def fwd_unit(w_ref, h_ref, z_ref, m_ref, s_ref, t_ref, tgt):
    rows = w_ref.shape[0]
    h = h_ref[...]
    tj = tgt - lax.broadcasted_iota(I32, (8, BT), 0)
    m, s, t = m_ref[...], s_ref[...], t_ref[...]
    for r0, rc in chunks(rows):
        z = lax.dot_general(w_ref[r0:r0 + rc, :], h, (((1,), (1,)), ((), ())), preferred_element_type=F32) * LOG2E
        z_ref[r0:r0 + rc, :] = z
        z = z.reshape(rc // 8, 8, BT)
        mn = jnp.maximum(m, jnp.max(z, axis=0))
        s = s * jnp.exp2(m - mn) + jnp.sum(jnp.exp2(z - mn[None]), axis=0)
        m = mn
        for k in range(rc // 8):
            t = jnp.where(tj == r0 + 8 * k, z[k], t)
    m_ref[...], s_ref[...], t_ref[...] = m, s, t


def bwd_unit(z_ref, lse, tgt, inv, wt_ref, h_ref, dw_ref, dh_ref):
    rows = z_ref.shape[0]
    h = h_ref[...]
    tj = tgt - lax.broadcasted_iota(I32, (8, BT), 0)
    acc = None
    for r0, rc in chunks(rows):
        z = z_ref[r0:r0 + rc, :].reshape(rc // 8, 8, BT)
        p = jnp.exp2(z - lse[None])
        row = lax.broadcasted_iota(I32, (rc // 8, 8, BT), 0) * 8 + r0
        dz = jnp.where(row == tj[None], p - inv, p).reshape(rc, BT)
        rk, rm = up(rc, 256), up(rc, 16)
        if rk > rc:
            dz = jnp.concatenate([dz, jnp.zeros((rk - rc, BT), F32)], axis=0)
        dz = dz.astype(BF16)
        d = jnp.dot(dz[:rm], h, preferred_element_type=F32)
        dw_ref[r0:r0 + rc, :] += d[:rc]
        d = jnp.dot(wt_ref[:, r0:r0 + rk], dz, preferred_element_type=F32)
        acc = d if acc is None else acc + d
    dh_ref[...] += acc


def fwd_kernel(n_half, n_blk, w0, w1, hbuf, tgt, base, z, st, wv, hv, zv, m, s, t, w_sem, h_sem, z_sem):
    rows = wv.shape[1]
    n_units = n_half * n_blk
    for k in range(n_half):
        src = (w0, w1)[k // 2]
        pltpu.make_async_copy(src.at[pl.ds((k % 2) * rows, rows)], wv.at[k], w_sem.at[k]).start()

    def load_h(u, slot):
        return pltpu.make_async_copy(hbuf.at[lax.rem(u, n_blk)], hv.at[slot], h_sem.at[slot])

    def store_z(u, slot):
        return pltpu.make_async_copy(zv.at[slot], z.at[u // n_blk, lax.rem(u, n_blk)], z_sem.at[slot])

    load_h(0, 0).start()
    m[...] = jnp.full_like(m, -jnp.inf)
    s[...] = jnp.zeros_like(s)
    t[...] = jnp.zeros_like(t)

    @pl.loop(0, n_units)
    def _(u):
        slot = lax.rem(u, 2)
        half, blk = u // n_blk, lax.rem(u, n_blk)

        @pl.when(blk == 0)
        def _():
            pltpu.make_async_copy(w0.at[pl.ds(0, rows)], wv.at[half], w_sem.at[half]).wait()

        load_h(u, slot).wait()

        @pl.when(u + 1 < n_units)
        def _():
            load_h(u + 1, 1 - slot).start()

        @pl.when(u >= 2)
        def _():
            store_z(u - 2, slot).wait()

        fwd_unit(wv.at[half], hv.at[slot], zv.at[slot], m.at[blk], s.at[blk], t.at[blk], tgt[blk] - base[half])
        store_z(u, slot).start()

    m1 = jnp.max(m[...], axis=1, keepdims=True)
    st[0] = m1[:, 0, :]
    st[1] = jnp.sum(s[...] * jnp.exp2(m[...] - m1), axis=1)
    st[2] = jnp.sum(t[...], axis=1)
    store_z(n_units - 2, 0).wait()
    store_z(n_units - 1, 1).wait()


def bwd_kernel(n_half, n_blk, inv, w0, w1, hbuf, tgt, base, lse, z, dw, dh, wv, wt, hv, zv, dwa, dha, w_sem, h_sem, z_sem, o_sem):
    rows = zv.shape[1]
    cols = wt.shape[2]
    n_units = n_half * n_blk

    def load_w(k):
        src = (w0, w1)[k // 2]
        return pltpu.make_async_copy(src.at[pl.ds((k % 2) * rows, rows)], wv, w_sem)

    def load_h(u, slot):
        return pltpu.make_async_copy(hbuf.at[u // n_half], hv.at[slot], h_sem.at[slot])

    def load_z(u, slot):
        return pltpu.make_async_copy(z.at[lax.rem(u, n_half), u // n_half], zv.at[slot], z_sem.at[slot])

    load_z(0, 0).start()
    load_h(0, 0).start()
    for k in range(n_half):
        load_w(k).start()
        load_w(k).wait()
        for r0, rc in chunks(rows):
            wt[k, :, r0:r0 + rc] = wv[r0:r0 + rc, :].T
        if cols > rows:
            wt[k, :, rows:] = jnp.zeros((wt.shape[1], cols - rows), BF16)
    dwa[...] = jnp.zeros_like(dwa)

    @pl.loop(0, n_units)
    def _(u):
        slot = lax.rem(u, 2)
        half, blk = lax.rem(u, n_half), u // n_half
        hslot = lax.rem(blk, 2)
        load_z(u, slot).wait()

        @pl.when(u + 1 < n_units)
        def _():
            load_z(u + 1, 1 - slot).start()

        @pl.when(half == 0)
        def _():
            pltpu.make_async_copy(hbuf.at[blk], hv.at[hslot], h_sem.at[hslot]).wait()

            @pl.when(blk + 1 < n_blk)
            def _():
                pltpu.make_async_copy(hbuf.at[blk + 1], hv.at[1 - hslot], h_sem.at[1 - hslot]).start()

            @pl.when(blk >= 2)
            def _():
                pltpu.make_async_copy(dha.at[hslot], dh.at[blk], o_sem.at[hslot]).wait()

            dha[hslot] = jnp.zeros(dha.shape[1:], F32)

        bwd_unit(zv.at[slot], lse[blk], tgt[blk] - base[half], inv, wt.at[half], hv.at[hslot], dwa.at[half], dha.at[hslot])

        @pl.when(half == n_half - 1)
        def _():
            pltpu.make_async_copy(dha.at[hslot], dh.at[blk], o_sem.at[hslot]).start()

    for k in range(2):
        pltpu.make_async_copy(dha.at[k], dh.at[0], o_sem.at[k]).wait()
    pltpu.make_async_copy(dwa, dw, w_sem).start()
    pltpu.make_async_copy(dwa, dw, w_sem).wait()


def solution(mesh):
    group_size = mesh.shape['fsdp']
    n_chips = group_size // 2
    quads = [list(range(q, q + 4)) for q in range(0, group_size, 4)]

    def vocab_peer(f):
        chip, core = f // 2, f % 2
        other = (chip + 1) % n_chips if chip % 2 else (chip - 1) % n_chips
        return other * 2 + core

    peer_perm = [(f, vocab_peer(f)) for f in range(group_size)]

    def local_head(hidden, targets, w_loc):
        n_micro, tok_dev, dim = hidden.shape
        vb = w_loc.shape[0]
        tokens = tok_dev * group_size
        rows = vb // 2
        n_own = n_micro * tok_dev // BT
        n_blk, n_half = 4 * n_own, 4
        me = lax.axis_index('fsdp')
        chip, core = me // 2, lax.rem(me, 2)
        step = 2 * lax.rem(chip, 2) - 1
        peer = lax.rem(chip + step + n_chips, n_chips) * 2 + core
        base = jnp.stack([me * vb, me * vb + rows, peer * vb, peer * vb + rows]).astype(I32)

        hbuf = lax.all_gather(hidden.reshape(n_own, BT, dim), 'fsdp', axis_index_groups=quads, tiled=True)
        tgt = lax.all_gather(targets.reshape(n_own, 1, BT), 'fsdp', axis_index_groups=quads, tiled=True)
        w_peer = lax.ppermute(w_loc, 'fsdp', peer_perm)

        z, st = pl.pallas_call(
            functools.partial(fwd_kernel, n_half, n_blk),
            out_shape=(jax.ShapeDtypeStruct((n_half, n_blk, rows, BT), F32), jax.ShapeDtypeStruct((3, n_blk, BT), F32)),
            in_specs=[ANY, ANY, ANY, VM, pl.BlockSpec(memory_space=pltpu.SMEM)],
            out_specs=(ANY, VM),
            scratch_shapes=[
                pltpu.VMEM((n_half, rows, dim), BF16), pltpu.VMEM((2, BT, dim), BF16), pltpu.VMEM((2, rows, BT), F32),
                pltpu.VMEM((n_blk, 8, BT), F32), pltpu.VMEM((n_blk, 8, BT), F32), pltpu.VMEM((n_blk, 8, BT), F32),
                pltpu.SemaphoreType.DMA((n_half,)), pltpu.SemaphoreType.DMA((2,)), pltpu.SemaphoreType.DMA((2,))],
            compiler_params=pltpu.CompilerParams(vmem_limit_bytes=VMEM_LIMIT), name='fwd',
        )(w_loc, w_peer, hbuf, tgt, base)

        sts = lax.all_gather(st, 'fsdp', axis_index_groups=quads)
        mx = jnp.max(sts[:, 0], axis=0)
        lse2 = mx + jnp.log2(jnp.sum(sts[:, 1] * jnp.exp2(sts[:, 0] - mx[None]), axis=0))
        tl = jnp.sum(sts[:, 2], axis=0)
        tok_loss = ((lse2 - tl) * LN2).reshape(4, n_micro, tok_dev)
        mine = lax.dynamic_index_in_dim(tok_loss, lax.rem(me, 4), 0, keepdims=False)
        loss = lax.psum(jnp.sum(mine, axis=1) / tokens, 'fsdp')
        lse_t = (lse2 + jnp.log2(jnp.float32(tokens))).reshape(n_blk, 1, BT)

        dw, dh = pl.pallas_call(
            functools.partial(bwd_kernel, n_half, n_blk, 1.0 / tokens),
            out_shape=(jax.ShapeDtypeStruct((n_half, rows, dim), F32), jax.ShapeDtypeStruct((n_blk, dim, BT), F32)),
            in_specs=[ANY, ANY, ANY, VM, pl.BlockSpec(memory_space=pltpu.SMEM), VM, ANY],
            out_specs=(ANY, ANY),
            scratch_shapes=[
                pltpu.VMEM((rows, dim), BF16), pltpu.VMEM((n_half, dim, up(rows, 256)), BF16), pltpu.VMEM((2, BT, dim), BF16),
                pltpu.VMEM((2, rows, BT), F32), pltpu.VMEM((n_half, rows, dim), F32), pltpu.VMEM((2, dim, BT), F32),
                pltpu.SemaphoreType.DMA, pltpu.SemaphoreType.DMA((2,)), pltpu.SemaphoreType.DMA((2,)), pltpu.SemaphoreType.DMA((2,))],
            compiler_params=pltpu.CompilerParams(vmem_limit_bytes=VMEM_LIMIT), name='bwd',
        )(w_loc, w_peer, hbuf, tgt, base, lse_t, z)

        dw = dw.reshape(2, vb, dim)
        d_w = dw[0] + lax.ppermute(dw[1], 'fsdp', peer_perm)
        d_h = lax.psum_scatter(dh, 'fsdp', axis_index_groups=quads, tiled=True)
        d_h = d_h.transpose(0, 2, 1).reshape(n_micro, tok_dev, dim)
        return loss, d_h, d_w

    return jax.shard_map(local_head, mesh=mesh,
                         in_specs=(P(None, ('dp', 'fsdp'), None), P(None, ('dp', 'fsdp')), P('fsdp', None)),
                         out_specs=(P('dp'), P(None, ('dp', 'fsdp'), None), P(('dp', 'fsdp'), None)),
                         check_vma=False)
```

time: 2110 us -> 982 us (0.47)
  matrix products: 881 us -> 0 us
  Pallas kernels: 0 us -> 517 us
  waiting for transfers between devices: 705 us -> 212 us
  other arithmetic: 172 us -> 12.6 us
  starting transfers between devices: 150 us -> 6.93 us
  blocking collectives: 98.6 us -> 198 us
  local copies, waits for them, and re-layouts: 78.6 us -> 20.9 us
    dot_general x31 -> x0, matrix products: 881 us -> none  [the longest x15 449 us: block_logits(): lax.dot_general(tok_rows, w_blk, (((1,), (1,)), ((), ())), preferred_elem...]
    ppermute x22 -> x2, waiting for transfers between devices: 705 us -> 81.3 us  [the longest x1 81.3 us: local_head(): w_peer = lax.ppermute(w_loc, 'fsdp', peer_perm)]
    pallas_call x0 -> x2, Pallas kernels: none -> 517 us  [the longest x1 313 us: local_head(): pl.pallas_call(functools.partial(bwd_kernel, n_half, n_blk, 1.0 / tokens)...]
    reduce_sum x9 -> x3, other arithmetic: 171 us -> 0.21 us  [the longest x1 0.14 us: local_head(): loss = lax.psum(jnp.sum(mine, axis=1) / tokens, 'fsdp')]
    ppermute x22 -> x2, starting transfers between devices: 150 us -> 6.8 us  [the longest x1 3.78 us: local_head(): w_peer = lax.ppermute(w_loc, 'fsdp', peer_perm)]
    psum x1, blocking collectives: 98.6 us -> 184 us  [local_head(): loss = lax.psum(jnp.sum(mine, axis=1) / tokens, 'fsdp')]
    reduce_scatter x0 -> x1, waiting for transfers between devices: none -> 69.9 us  [local_head(): d_h = lax.psum_scatter(dh, 'fsdp', axis_index_groups=quads, tiled=True)]
    while x21 -> x0, local copies, waits for them, and re-layouts: 61.4 us -> none
  transfers between devices with their start and end apart: 22 -> 4, of which waited for: 21 -> 3; matrix products, arithmetic and copies ran while one was open for 21% -> 2% of each run, Pallas kernels for 0% -> 0%
where the time goes in v1:
time: 982 us
  Pallas kernels  517 us (53%)
  waiting for transfers between devices  212 us (22%)
  blocking collectives  198 us (20%)
  local copies, waits for them, and re-layouts  20.9 us (2%)
  between operations  14.1 us (1%)
  other arithmetic  12.6 us (1%)
    pallas_call x1, Pallas kernels, local_head(): pl.pallas_call(functools.partial(bwd_kernel, n_half, n_blk, 1.0 / tokens)...  313 us
    pallas_call x1, Pallas kernels, local_head(): pl.pallas_call(functools.partial(fwd_kernel, n_half, n_blk), out_shape=(j...  204 us
    psum x1, blocking collectives, local_head(): loss = lax.psum(jnp.sum(mine, axis=1) / tokens, 'fsdp')  184 us
    ppermute x1, waiting for transfers between devices, local_head(): w_peer = lax.ppermute(w_loc, 'fsdp', peer_perm)  81.3 us
    reduce_scatter x1, waiting for transfers between devices, local_head(): d_h = lax.psum_scatter(dh, 'fsdp', axis_index_groups=quads, tiled=True)  69.9 us
    all_gather x1, waiting for transfers between devices, local_head(): lax.all_gather(hidden.reshape(n_own, BT, dim), 'fsdp', axis_index_groups=...  60.5 us
  transfers between devices with their start and end apart: 4, of which 3 were waited for; matrix products, arithmetic and copies ran while one was open for 2% of the time, Pallas kernels for 0%

profile of v1, /device:TPU:113, one launch (start us, length us, event | category | flops | bytes accessed | tf_op | source)
XLA Modules:
  0.0 982.0 jit_solution(12346216429345588890)
XLA Ops:
  7.2 0.1 all-gather.3.cloned.1.call-start
  7.2 0.7 all-gather.3.cloned.1.call-update
  8.0 0.1 reduce-scatter.2.cloned.1.call-start
  8.0 3.8 collective-permute-start
  11.8 0.7 reshape.58
  12.6 6.0 all_gather.13.tgt
  18.6 0.7 pad_add_fusion.base
  19.2 81.3 %collective-permute-done.w1 = bf16[4016,512]{1,0:T(8,128)(2,1)} collective-permute-done((bf16[4016,512]{1,0:T(8,128)(2,1)}, bf16[4016,512]{1,0:T(8,128)(2,1)}, u32[]{:S(2)}, u32[]{:S(2)}) %collective-permute-start) | collective-permute-done | bytes 4112416 | tf_op jit(solution)/shard_map/ppermute | solution.py:204
  100.5 60.5 %all-gather.3.cloned.1.call-done.hbuf = bf16[16,1024,512]{2,1,0:T(8,128)(2,1)} async-done(((bf16[4,1024,512]{2,1,0:T(8,128)(2,1)}), bf16[16,1024,512]{2,1,0:T(8,128)(2,1)}) %all-gather.3.cloned.1.call-update) | async-done | bytes 16777232 | tf_op jit(solution)/shard_map/all_gather | solution.py:202
  161.0 204.2 %fwd.1 = (f32[4,16,2008,1024]{3,2,1,0:T(8,128)}, f32[3,16,1024]{2,1,0:T(8,128)}) custom-call(bf16[4016,512]{1,0:T(8,128)(2,1)} %w0.3, bf16[4016,512]{1,0:T(8,128)(2,1)} %collective-permute-done.w1, bf16[16,1024,512]{2,1,0:T(8,128)(2,1)} %all-gather.3.cloned.1.call-done.hbuf, s32[16,1,1024]{2,1,0:T(1,128)} %all_gather.13.tgt, s32[4]{0:T(128)} %pad_add_fusion.base), custom_call_target="tpu_custom_call" | custom-call | tf_op jit(solution)/shard_map/fwd/pallas_call | solution.py:206
  365.2 7.7 all-gather
  373.0 0.1 fusion.1
  373.1 0.7 broadcast_add_fusion
  373.7 0.7 add.66.lse
  374.4 313.0 %bwd.1 = (f32[4,2008,512]{2,1,0:T(8,128)}, f32[16,512,1024]{2,1,0:T(8,128)}) custom-call(bf16[4016,512]{1,0:T(8,128)(2,1)} %w0.3, bf16[4016,512]{1,0:T(8,128)(2,1)} %collective-permute-done.w1, bf16[16,1024,512]{2,1,0:T(8,128)(2,1)} %all-gather.3.cloned.1.call-done.hbuf, s32[16,1,1024]{2,1,0:T(1,128)} %all_gather.13.tgt, s32[4]{0:T(128)} %pad_add_fusion.base, ...), custom_call_target="tpu_custom_call" | custom-call | tf_op jit(solution)/shard_map/bwd/pallas_call | solution.py:227
  687.4 0.1 reduce-scatter.2.cloned.1.call-update
  687.4 0.0 copy-start
  687.4 10.8 %fusion.4 = (f32[2,2008,512]{2,1,0:T(8,128)}, f32[2,2008,512]{2,1,0:T(8,128)}) fusion(f32[4,2008,512]{2,1,0:T(8,128)} %get-tuple-element.10), kind=kLoop, calls=%fused_computation.15 | loop fusion | bytes 32899072 | tf_op jit(solution)/shard_map/slice | solution.py:240
  698.2 3.0 collective-permute-start.1
  701.2 0.0 copy-done
  701.3 0.1 dynamic-slice_reduce_fusion
  701.4 184.1 %psum.7 = f32[2]{0:T(128)} all-reduce(f32[2]{0:T(128)S(1)} %broadcast_multiply_fusion), channel_id=1, replica_groups=mesh['dp'=2,'fsdp'=8] {'fsdp'}, use_global_device_ids=true, to_apply=%region_4.5 | all-reduce | flops 2 | bytes 16 | tf_op jit(solution)/shard_map/psum | solution.py:224
  885.5 0.0 collective-permute-done.1
  885.5 11.1 %bitcast_add_fusion = f32[4016,512]{1,0:T(8,128)} fusion(f32[4016,512]{1,0:T(8,128)} %collective-permute-done.1, f32[2,2008,512]{2,1,0:T(8,128)} %get-tuple-element.11), kind=kLoop, calls=%fused_computation | loop fusion | flops 2056192 | bytes 24674304 | tf_op jit(solution)/shard_map/add | solution.py:240
  896.6 69.9 %reduce-scatter.2.cloned.1.call-done = f32[4,512,1024]{2,1,0:T(8,128)} async-done(((f32[16,512,1024]{2,1,0:T(8,128)}), f32[4,512,1024]{2,1,0:T(8,128)}) %reduce-scatter.2.cloned.1.call-update) | async-done | bytes 8388624 | tf_op jit(solution)/shard_map/reduce_scatter | solution.py:241
  966.5 8.7 copy.10
  (4 shorter events, 0.1 us)
Async XLA Ops:
  7.2 153.9 %all-gather.3.cloned.1.call-start = ((), (), s32[]{:S(2)}) async-start(), calls=%async_computation.1 | async-start | bytes 20971520 | tf_op jit(solution)/shard_map/all_gather | solution.py:202
  8.0 958.5 %reduce-scatter.2.cloned.1.call-start = ((), (), s32[]{:S(2)}) async-start(), calls=%async_computation.2 | async-start | bytes 41943040 | tf_op jit(solution)/shard_map/reduce_scatter | solution.py:241
  8.0 92.5 %collective-permute-start = (bf16[4016,512]{1,0:T(8,128)(2,1)}, bf16[4016,512]{1,0:T(8,128)(2,1)}, u32[]{:S(2)}, u32[]{:S(2)}) collective-permute-start(bf16[4016,512]{1,0:T(8,128)(2,1)} %w0.3), channel_id=1, source_target_pairs={{0,6},{1,7},{2,4},{3,5},{4,2},{5,3},{6,0},{7,1},{8,14},{9,15},{10,... | collective-permute-start | bytes 12337160 | tf_op jit(solution)/shard_map/ppermute | solution.py:204
  687.4 13.8 %copy-start = (f32[16,1024]{1,0:T(8,128)S(1)}, f32[16,1024]{1,0:T(8,128)}, u32[]{:S(2)}) copy-start(f32[16,1024]{1,0:T(8,128)} %get-tuple-element.14) | copy-start | bytes 196612
  698.2 187.3 %collective-permute-start.1 = (f32[4016,512]{1,0:T(8,128)}, f32[4016,512]{1,0:T(8,128)}, u32[]{:S(2)}, u32[]{:S(2)}) collective-permute-start(f32[4016,512]{1,0:T(8,128)} %bitcast.11), channel_id=1, source_target_pairs={{0,6},{1,7},{2,4},{3,5},{4,2},{5,3},{6,0},{7,1},{8,14},{9,15},{10,... | collective-permute-start | bytes 24674312 | tf_op jit(solution)/shard_map/ppermute | solution.py:240
Sparse Core Ops, SparseCore 0:
  9.6 151.4 all-gather.2
  687.6 278.8 reduce-scatter.1

commit v2 on v0

v2 whole, which is shorter than its diff:
```python
import functools
import math

import jax
import jax.numpy as jnp
from jax import lax
from jax.experimental import pallas as pl
from jax.experimental.pallas import tpu as pltpu
from jax.sharding import PartitionSpec as P

F32, BF16, I32 = jnp.float32, jnp.bfloat16, jnp.int32
LOG2E = 1.4426950408889634
LN2 = 0.6931471805599453
BT = 1024
RC = 256
VMEM_LIMIT = 61 << 20
ANY = pl.BlockSpec(memory_space=pl.ANY)
VM = pl.BlockSpec(memory_space=pltpu.VMEM)
DMA = pltpu.SemaphoreType.DMA
local = pltpu.make_async_copy


def remote(src, dst, send_sem, recv_sem, to):
    return pltpu.make_async_remote_copy(src_ref=src, dst_ref=dst, send_sem=send_sem, recv_sem=recv_sem,
                                        device_id={'fsdp': to}, device_id_type=pl.DeviceIdType.MESH)


def chunks(rows):
    return [(r0, min(RC, rows - r0)) for r0 in range(0, rows, RC)]


def up(a, b):
    return -(-a // b) * b


def pick(x, segments):
    out = segments[0][1]
    for lo, vals in segments[1:]:
        out = tuple(jnp.where(x >= lo, a, b) for a, b in zip(vals, out))
    return out


class Place:
    def __init__(self, n):
        self.me = lax.axis_index('fsdp')
        self.chip, self.core = self.me // 2, lax.rem(self.me, 2)
        self.odd = lax.rem(self.chip, 2)
        self.sib = self.me + 1 - 2 * self.core
        self.par = self.me + 2 - 4 * self.odd
        self.diag = self.sib + 2 - 4 * self.odd
        self.peer = lax.rem(self.chip + 2 * self.odd - 1 + n // 2, n // 2) * 2 + self.core

    def share(self, r):
        a, b = lax.rem(r, 2), r // 2
        return 2 * (self.odd + b - 2 * self.odd * b) + self.core + a - 2 * self.core * a


def barrier_with(others):
    sem = pltpu.get_barrier_semaphore()
    for d in others:
        pl.semaphore_signal(sem, inc=1, device_id={'fsdp': d}, device_id_type=pl.DeviceIdType.MESH)
    pl.semaphore_wait(sem, len(others))


def fwd_unit(w_ref, h_ref, z_ref, m_ref, s_ref):
    rows = w_ref.shape[0]
    h = h_ref[...]
    m, s = m_ref[...], s_ref[...]
    for r0, rc in chunks(rows):
        z = lax.dot_general(w_ref[r0:r0 + rc, :], h, (((1,), (1,)), ((), ())), preferred_element_type=F32) * LOG2E
        z_ref[r0:r0 + rc, :] = z
        z = z.reshape(rc // 8, 8, BT)
        mn = jnp.maximum(m, jnp.max(z, axis=0))
        s = s * jnp.exp2(m - mn) + jnp.sum(jnp.exp2(z - mn[None]), axis=0)
        m = mn
    m_ref[...], s_ref[...] = m, s


def bwd_unit(z_ref, lse, tgt, inv, wt_ref, h_ref, dw_ref, dh_ref, tl_ref):
    rows = z_ref.shape[0]
    h = h_ref[...]
    tj = tgt - lax.broadcasted_iota(I32, (8, BT), 0)
    tl = jnp.zeros((8, BT), F32)
    acc = None
    for r0, rc in chunks(rows):
        z = z_ref[r0:r0 + rc, :].reshape(rc // 8, 8, BT)
        p = jnp.exp2(z - lse[None])
        hit = lax.broadcasted_iota(I32, (rc // 8, 8, BT), 0) * 8 + r0 == tj[None]
        dz = jnp.where(hit, p - inv, p).reshape(rc, BT)
        for k in range(rc // 8):
            tl = jnp.where(hit[k], z[k], tl)
        rk, rm = up(rc, 256), up(rc, 16)
        if rk > rc:
            dz = jnp.concatenate([dz, jnp.zeros((rk - rc, BT), F32)], axis=0)
        dz = dz.astype(BF16)
        d = jnp.dot(dz[:rm], h, preferred_element_type=F32)
        dw_ref[r0:r0 + rc, :] += d[:rc]
        d = jnp.dot(wt_ref[:, r0:r0 + rk], dz, preferred_element_type=F32)
        acc = d if acc is None else acc + d
    dh_ref[...] += acc
    tl_ref[...] += tl


def fwd_kernel(n, tokens, hid, w, tg, z, lse, hbuf, wpeer, tall, wv, hv, zv, m, s, st, strx,
               rh, lw, rw, sw, shs, shp, sf, stt, rt, lt, oh, ow, oz, ss, rs):
    at = Place(n)
    n_own = hid.shape[0]
    rows = wv.shape[1]
    quad = (at.me, at.sib, at.par, at.diag)

    def blk(r, b):
        return n_own * at.share(r) + b

    half_src = [w.at[pl.ds(k * rows, rows)] for k in range(2)]
    for k in range(2):
        local(half_src[k], wv.at[k], lw.at[k]).start()
    for b in range(n_own):
        local(hid.at[b], hv.at[blk(0, b)], rh.at[b]).start()
    own_t = tall.at[pl.ds(n_own * at.share(0), n_own)]
    local(tg, own_t, lt).start()

    barrier_with([at.sib, at.par, at.diag, at.peer])

    def send_sib(b):
        return remote(hid.at[b], hv.at[blk(0, b)], shs.at[b], rh.at[n_own + b], at.sib)

    def send_par(b):
        return remote(hid.at[b], hv.at[blk(0, b)], shp.at[b], rh.at[2 * n_own + b], at.par)

    def forward(b):
        return remote(hv.at[blk(2, b)], hv.at[blk(2, b)], sf.at[b], rh.at[3 * n_own + b], at.sib)

    def send_w(k):
        return remote(half_src[k], wv.at[2 + k], sw.at[k], rw.at[k], at.peer)

    def send_t(r):
        return remote(tg, own_t, stt.at[r - 1], rt.at[r - 1], quad[r])

    def send_st(r):
        return remote(st, strx.at[r - 1], ss.at[r - 1], rs.at[r - 1], quad[r])

    for k in range(n_own):
        send_sib(k).start()
        send_par(k).start()
        if k < 2:
            send_w(k).start()
    for r in range(1, 4):
        send_t(r).start()

    m[...] = jnp.full_like(m, -jnp.inf)
    s[...] = jnp.zeros_like(s)

    n1 = 4 * n_own
    def order(u):
        def near(q):
            return lax.rem(q, 2), q // (2 * n_own), lax.rem(q // 2, n_own)

        def far(q, b0):
            return lax.rem(q, 2), 2 + lax.rem(q // 2, 2), b0 + q // 4

        def wide(q, h):
            return jnp.full_like(q, h), q // n_own, lax.rem(q, n_own)

        s2, s3 = n1, n1 + 4
        s4 = s3 + 2 * n_own
        s5 = s4 + 4 * (n_own - 2)
        s6 = s5 + 2 * n_own
        s7 = s6 + 4
        h7, r7, b7 = far(u - s7, 0)
        return pick(u, [(0, near(u)), (s2, far(u - s2, 0)), (s3, wide(u - s3, 2)), (s4, far(u - s4, 1)),
                        (s5, wide(u - s5, 3)), (s6, far(u - s6, n_own - 1)), (s7, (h7 + 2, r7, b7))]), s3, s5

    n_units = 4 * 4 * n_own

    def store_z(u):
        (h, r, b), _, _ = order(u)
        slot = lax.rem(u, 3)
        return local(zv.at[slot], z.at[h, blk(r, b)], oz.at[slot])

    def wait_z(slot):
        local(zv.at[slot], z.at[0, 0], oz.at[slot]).wait()

    @pl.loop(0, n_units)
    def _(u):
        slot = lax.rem(u, 3)
        (h, r, b), first2, first3 = order(u)
        i = blk(r, b)

        @pl.when(u < 2)
        def _():
            local(half_src[0], wv.at[u], lw.at[u]).wait()

        @pl.when(jnp.logical_or(u == first2, u == first3))
        def _():
            remote(half_src[0], wv.at[h], sw.at[0], rw.at[h - 2], at.peer).wait_recv()
            local(wv.at[h], wpeer.at[h - 2], ow.at[h - 2]).start()

        @pl.when(h == 0)
        def _():
            @pl.when(r == 0)
            def _():
                local(hid.at[0], hv.at[i], rh.at[b]).wait()

            @pl.when(r > 0)
            def _():
                remote(hid.at[0], hv.at[i], shs.at[0], rh.at[n_own * r + b], at.sib).wait_recv()

            local(hv.at[i], hbuf.at[i], oh.at[i]).start()

            @pl.when(r == 2)
            def _():
                forward(b).start()

        @pl.when(u >= 3)
        def _():
            wait_z(slot)

        fwd_unit(wv.at[h], hv.at[i], zv.at[slot], m.at[i], s.at[i])
        store_z(u).start()

    mm = m[...]
    m1 = jnp.max(mm, axis=1, keepdims=True)
    st[0] = m1[:, 0, :]
    st[1] = jnp.sum(s[...] * jnp.exp2(mm - m1), axis=1)
    for r in range(1, 4):
        send_st(r).start()
    for r in range(1, 4):
        send_t(r).wait()
        send_st(r).wait()
    mx = st[0]
    for r in range(3):
        mx = jnp.maximum(mx, strx[r, 0])
    tot = st[1] * jnp.exp2(st[0] - mx)
    for r in range(3):
        tot = tot + strx[r, 1] * jnp.exp2(strx[r, 0] - mx)
    lse[...] = (mx + jnp.log(tot) * LOG2E + math.log2(tokens)).reshape(lse.shape)

    local(tg, own_t, lt).wait()
    for k in range(n_own):
        send_sib(k).wait_send()
        send_par(k).wait_send()
        forward(k).wait_send()
    for k in range(2):
        send_w(k).wait_send()
        local(wv.at[2 + k], wpeer.at[k], ow.at[k]).wait()
    for k in range(4 * n_own):
        local(hv.at[k], hbuf.at[k], oh.at[k]).wait()
    for k in range(3):
        wait_z(k)


def bwd_kernel(n, tokens, n_micro, w, wpeer, hbuf, tall, lse, z, dwo, rxw, dho, loss, part, rxs, txb, rxb, zblk,
               wv, wt, hv, zv, dwa, dha, rbuf, tla, lmsg, lrx,
               lw, lz, lh, li, lr, eo, es, rss, sb, rb, swr, rwr, sl, rl):
    at = Place(n)
    n_own = dho.shape[0]
    rows, cols = zv.shape[1], wt.shape[2]
    inv = 1.0 / tokens

    sem = pltpu.get_barrier_semaphore()
    for d in range(1, n):
        pl.semaphore_signal(sem, inc=1, device_id={'fsdp': lax.rem(at.me + d, n)}, device_id_type=pl.DeviceIdType.MESH)

    def blk(r, b):
        return n_own * at.share(r) + b

    far = 2 * (n_own - 1)
    v_b, v_c = 2, 2 + far + 2 * n_own
    v_d = v_c + far - 2
    v_e = v_d + 2 + 2 * n_own
    v_f = v_e + 2
    n_visits = v_f + 2 * n_own
    u_b = 8
    u_c = u_b + far + 2 * n_own
    u_d = u_c + 3 * (far - 2)
    u_e = u_d + 2 + 2 * n_own
    u_f = u_e + 4
    n_units = u_f + 4 * n_own

    def visit(v):
        def far_pair(q, b0):
            return 3 - lax.rem(q, 2), b0 + q // 2

        def near_pair(q):
            return 1 - lax.rem(q, 2), q // 2

        one = jnp.ones_like(v)
        zero = one - 1
        qb, qc, qd, qe, qf = v - v_b, v - v_c, v - v_d, v - v_e, v - v_f
        return pick(v, [
            (0, (4 * one, *far_pair(v, 0), zero, 4 * v, one, one)),
            (v_b, (one, *far_pair(qb, 1), 2 * one, u_b + qb, one, zero)),
            (v_b + far, (one, *near_pair(qb - far), 2 * one, u_b + qb, one, zero)),
            (v_c, (3 * one, *far_pair(qc, 1), 3 * one, u_c + 3 * qc, zero, one)),
            (v_d, (one, *far_pair(qd, n_own - 1), 3 * one, u_d + qd, zero, zero)),
            (v_d + 2, (one, *near_pair(qd - 2), 3 * one, u_d + qd, zero, zero)),
            (v_e, (2 * one, *far_pair(qe, n_own - 1), zero, u_e + 2 * qe, zero, one)),
            (v_f, (2 * one, *near_pair(qf), zero, u_f + 2 * qf, zero, one)),
        ])

    def load_z(h, i, slot):
        return local(z.at[h, i], zv.at[slot], lz.at[slot])

    def load_h(i, slot):
        return local(hbuf.at[i], hv.at[slot], lh.at[slot])

    def start_init(i, fresh, slot):
        @pl.when(fresh == 1)
        def _():
            local(zblk, dha.at[slot], li.at[slot]).start()

        @pl.when(fresh == 0)
        def _():
            local(part.at[i], dha.at[slot], li.at[slot]).start()

    def to_sib(r, b, slot):
        return remote(dha.at[slot], rxs.at[n_own * (1 - r // 2) + b], es.at[slot], rss.at[n_own * (1 - r // 2) + b], at.sib)

    def from_sib(r, b):
        return remote(dha.at[0], rxs.at[n_own * (1 - r // 2) + b], es.at[0], rss.at[n_own * (1 - r // 2) + b], at.sib)

    def to_par(b):
        return remote(txb.at[b], rxb.at[b], sb.at[b], rb.at[b], at.par)

    def to_peer(k):
        return remote(dwa.at[2 + k], rxw.at[k], swr.at[k], rwr.at[k], at.peer)

    load_z(0, blk(3, 0), 0).start()
    load_h(blk(3, 0), 0).start()
    rbuf[0] = jnp.zeros(rbuf.shape[1:], F32)
    local(rbuf.at[0], zblk, lr.at[0]).start()
    halves = [w.at[pl.ds(0, rows)], w.at[pl.ds(rows, rows)], wpeer.at[0], wpeer.at[1]]
    local(halves[0], wv.at[0], lw.at[0]).start()
    dwa[...] = jnp.zeros_like(dwa)
    tla[...] = jnp.zeros_like(tla)
    for k in range(4):
        local(halves[k], wv.at[k % 2], lw.at[k % 2]).wait()
        if k < 3:
            local(halves[k + 1], wv.at[(k + 1) % 2], lw.at[(k + 1) % 2]).start()
        for r0, rc in chunks(rows):
            wt[k, :, r0:r0 + rc] = wv[k % 2, r0:r0 + rc, :].T
        if cols > rows:
            wt[k, :, rows:] = jnp.zeros((wt.shape[1], cols - rows), BF16)
    local(rbuf.at[0], zblk, lr.at[0]).wait()
    local(zblk, dha.at[0], li.at[0]).start()
    pl.semaphore_wait(sem, n - 1)

    def finish(v):
        slot = lax.rem(v, 3)
        _, r, b, _, _, _, comp = visit(v)
        sent = jnp.logical_and(comp == 1, lax.rem(r, 2) == 1)

        @pl.when(sent)
        def _():
            to_sib(r, b, slot).wait_send()

        @pl.when(jnp.logical_not(sent))
        def _():
            local(dha.at[slot], part.at[0], eo.at[slot]).wait()

        @pl.when(jnp.logical_and(comp == 1, r == 2))
        def _():
            to_par(b).start()

    @pl.loop(0, n_visits)
    def _(v):
        count, r, b, h0, u0, _, comp = visit(v)
        _, r_n, b_n, h0_n, _, fresh_n, _ = visit(v + 1)
        i, i_n = blk(r, b), blk(r_n, b_n)
        hs, ds = lax.rem(v, 2), lax.rem(v, 3)
        mine = jnp.logical_and(comp == 1, lax.rem(r, 2) == 0)
        last = jnp.logical_and(mine, r == 0)

        @pl.when(v >= 2)
        def _():
            finish(v - 2)

        local(zblk, dha.at[ds], li.at[ds]).wait()
        load_h(i, hs).wait()

        @pl.when(v + 1 < n_visits)
        def _():
            start_init(i_n, fresh_n, lax.rem(v + 1, 3))
            load_h(i_n, 1 - hs).start()

        @pl.loop(0, count)
        def _(k):
            u = u0 + k
            slot = lax.rem(u, 2)
            h = lax.rem(h0 + k, 4)
            end = k + 1 == count
            load_z(h, i, slot).wait()

            @pl.when(u + 1 < n_units)
            def _():
                load_z(jnp.where(end, h0_n, lax.rem(h + 1, 4)), jnp.where(end, i_n, i), 1 - slot).start()

            @pl.when(jnp.logical_and(end, mine))
            def _():
                from_sib(r, b).wait_recv()
                local(rxs.at[n_own * (1 - r // 2) + b], rbuf.at[0], lr.at[0]).start()

            @pl.when(jnp.logical_and(end, last))
            def _():
                to_par(b).wait_recv()
                local(rxb.at[b], rbuf.at[1], lr.at[1]).start()

            base = jnp.where(h < 2, at.me, at.peer) * (2 * rows) + lax.rem(h, 2) * rows
            bwd_unit(zv.at[slot], lse[i], tall[i] - base, inv, wt.at[h], hv.at[hs], dwa.at[h], dha.at[ds],
                     tla.at[b // (n_own // n_micro)])

        @pl.when(mine)
        def _():
            local(rxs.at[0], rbuf.at[0], lr.at[0]).wait()
            dha[ds] += rbuf[0]

        @pl.when(last)
        def _():
            local(rxb.at[0], rbuf.at[1], lr.at[1]).wait()
            dha[ds] += rbuf[1]
            local(dha.at[ds], dho.at[b], eo.at[ds]).start()

        @pl.when(jnp.logical_and(mine, r == 2))
        def _():
            local(dha.at[ds], txb.at[b], eo.at[ds]).start()

        @pl.when(jnp.logical_and(comp == 1, lax.rem(r, 2) == 1))
        def _():
            to_sib(r, b, ds).start()

        @pl.when(comp == 0)
        def _():
            local(dha.at[ds], part.at[i], eo.at[ds]).start()

        @pl.when(v == v_c - 1)
        def _():
            to_peer(0).start()

        @pl.when(v == v_e - 1)
        def _():
            to_peer(1).start()

    per = n_own // n_micro
    top = lax.broadcasted_iota(I32, (8, BT), 0) == 0
    for k in range(n_micro):
        tot = lse[blk(0, k * per)] - math.log2(tokens)
        for b in range(k * per + 1, (k + 1) * per):
            tot = tot + (lse[blk(0, b)] - math.log2(tokens))
        val = (jnp.where(top, tot, 0.0) - tla[k]) * (LN2 * inv)
        acc = val[:, :128]
        for c in range(128, BT, 128):
            acc = acc + val[:, c:c + 128]
        lmsg[k] = acc

    def send_loss(d):
        return remote(lmsg, lrx.at[d - 1], sl.at[d - 1], rl.at[d - 1], lax.rem(at.me + d, n))

    for d in range(1, n):
        send_loss(d).start()
    own_dw = local(dwa.at[pl.ds(0, 2)], dwo, lw.at[0])
    own_dw.start()
    finish(jnp.int32(n_visits - 2))
    finish(jnp.int32(n_visits - 1))
    for d in range(1, n):
        send_loss(d).wait()
    tot = lmsg[...]
    for d in range(n - 1):
        tot = tot + lrx[d]
    loss[...] = tot
    for k in range(2):
        to_peer(k).wait()
    for b in range(n_own):
        to_par(b).wait_send()
    own_dw.wait()


def solution(mesh):
    n = mesh.shape['fsdp']

    def local_head(hidden, targets, w_loc):
        n_micro, tok_dev, dim = hidden.shape
        vb = w_loc.shape[0]
        tokens = tok_dev * n
        rows = vb // 2
        n_own = n_micro * tok_dev // BT
        n_blk = 4 * n_own

        def out(shape, dtype=F32):
            return jax.ShapeDtypeStruct(shape, dtype)

        z, lse, hbuf, wpeer, tall = pl.pallas_call(
            functools.partial(fwd_kernel, n, tokens),
            out_shape=(out((4, n_blk, rows, BT)), out((n_blk, 1, BT)), out((n_blk, BT, dim), BF16), out((2, rows, dim), BF16),
                       out((n_blk, 1, BT), I32)),
            in_specs=[ANY, ANY, VM],
            out_specs=(ANY, VM, ANY, ANY, ANY),
            scratch_shapes=[
                pltpu.VMEM((4, rows, dim), BF16), pltpu.VMEM((n_blk, BT, dim), BF16), pltpu.VMEM((3, rows, BT), F32),
                pltpu.VMEM((n_blk, 8, BT), F32), pltpu.VMEM((n_blk, 8, BT), F32), pltpu.VMEM((2, n_blk, BT), F32),
                pltpu.VMEM((3, 2, n_blk, BT), F32),
                DMA((n_blk,)), DMA((2,)), DMA((2,)), DMA((2,)), DMA((n_own,)), DMA((n_own,)), DMA((n_own,)),
                DMA((3,)), DMA((3,)), DMA, DMA((n_blk,)), DMA((2,)), DMA((3,)), DMA((3,)), DMA((3,))],
            compiler_params=pltpu.CompilerParams(vmem_limit_bytes=VMEM_LIMIT, collective_id=0, has_side_effects=True),
            name='fwd',
        )(hidden.reshape(n_own, BT, dim), w_loc, targets.reshape(n_own, 1, BT))

        blk_shape = (dim, BT)
        dwo, rxw, dho, loss, *_ = pl.pallas_call(
            functools.partial(bwd_kernel, n, tokens, n_micro),
            out_shape=(out((2, rows, dim)), out((2, rows, dim)), out((n_own, *blk_shape)), out((n_micro, 8, 128)),
                       out((n_blk, *blk_shape)), out((2 * n_own, *blk_shape)), out((n_own, *blk_shape)), out((n_own, *blk_shape)),
                       out(blk_shape)),
            in_specs=[ANY, ANY, ANY, VM, VM, ANY],
            out_specs=(ANY, ANY, ANY, VM, ANY, ANY, ANY, ANY, ANY),
            scratch_shapes=[
                pltpu.VMEM((2, rows, dim), BF16), pltpu.VMEM((4, dim, up(rows, 256)), BF16), pltpu.VMEM((2, BT, dim), BF16),
                pltpu.VMEM((2, rows, BT), F32), pltpu.VMEM((4, rows, dim), F32), pltpu.VMEM((3, *blk_shape), F32),
                pltpu.VMEM((2, *blk_shape), F32), pltpu.VMEM((n_micro, 8, BT), F32), pltpu.VMEM((n_micro, 8, 128), F32),
                pltpu.VMEM((n - 1, n_micro, 8, 128), F32),
                DMA((2,)), DMA((2,)), DMA((2,)), DMA((3,)), DMA((2,)), DMA((3,)), DMA((3,)), DMA((2 * n_own,)),
                DMA((n_own,)), DMA((n_own,)), DMA((2,)), DMA((2,)), DMA((n - 1,)), DMA((n - 1,))],
            compiler_params=pltpu.CompilerParams(vmem_limit_bytes=VMEM_LIMIT, collective_id=1, has_side_effects=True),
            name='bwd',
        )(w_loc, wpeer, hbuf, tall, lse, z)

        d_w = (dwo + rxw).reshape(vb, dim)
        d_h = dho.transpose(0, 2, 1).reshape(n_micro, tok_dev, dim)
        return jnp.sum(loss, axis=(1, 2)), d_h, d_w

    return jax.shard_map(local_head, mesh=mesh,
                         in_specs=(P(None, ('dp', 'fsdp'), None), P(None, ('dp', 'fsdp')), P('fsdp', None)),
                         out_specs=(P('dp'), P(None, ('dp', 'fsdp'), None), P(('dp', 'fsdp'), None)),
                         check_vma=False)
```

time: 2110 us -> 535 us (0.25)
  matrix products: 881 us -> 0 us
  waiting for transfers between devices: 705 us -> 0 us
  Pallas kernels: 0 us -> 511 us
  other arithmetic: 172 us -> 12.4 us
  starting transfers between devices: 150 us -> 0 us
  blocking collectives: 98.6 us -> 0 us
  local copies, waits for them, and re-layouts: 78.6 us -> 10 us
    dot_general x31 -> x0, matrix products: 881 us -> none  [the longest x15 449 us: block_logits(): lax.dot_general(tok_rows, w_blk, (((1,), (1,)), ((), ())), preferred_elem...]
    ppermute x22 -> x0, waiting for transfers between devices: 705 us -> none  [the longest x7 304 us: fwd_body(): w_cur = lax.ppermute(w_cur, 'fsdp', shift_perm)]
    pallas_call x0 -> x2, Pallas kernels: none -> 511 us  [the longest x1 326 us: local_head(): pl.pallas_call(functools.partial(bwd_kernel, n, tokens, n_micro), out_sha...]
    reduce_sum x9 -> x1, other arithmetic: 171 us -> 1.3 us  [local_head(): return (jnp.sum(loss, axis=(1, 2)), d_h, d_w)]
    ppermute x22 -> x0, starting transfers between devices: 150 us -> none  [the longest x7 85.1 us: bwd_body(): w_cur = lax.ppermute(w_cur, 'fsdp', shift_perm)]
    psum x1 -> x0, blocking collectives: 98.6 us -> none  [local_head(): lax.psum(jnp.sum((log_norm - tgt_logit).reshape(n_micro, tok_dev), axis=1...]
    while x21 -> x0, local copies, waits for them, and re-layouts: 61.4 us -> none
  transfers between devices with their start and end apart: 22 -> 0, of which waited for: 21 -> 0; matrix products, arithmetic and copies ran while one was open for 21% -> 0% of each run, Pallas kernels for 0% -> 0%
where the time goes in v2:
time: 535 us; the launch traced here: 534 us
  Pallas kernels  511 us (96%)
  other arithmetic  12.4 us (2%)
  local copies, waits for them, and re-layouts  10 us (2%)
    pallas_call x1, Pallas kernels, local_head(): pl.pallas_call(functools.partial(bwd_kernel, n, tokens, n_micro), out_sha...  326 us
    pallas_call x1, Pallas kernels, local_head(): pl.pallas_call(functools.partial(fwd_kernel, n, tokens), out_shape=(out((...  185 us
    add x1, other arithmetic, local_head(): d_w = (dwo + rxw).reshape(vb, dim)  11.1 us

profile of v2, /device:TPU:113, one launch (start us, length us, event | category | flops | bytes accessed | tf_op | source)
XLA Modules:
  0.0 534.2 jit_solution(4232528224738072154)
XLA Ops:
  0.6 1.4 reshape.19.tg
  2.0 185.2 %fwd.1 = (f32[4,16,2008,1024]{3,2,1,0:T(8,128)}, f32[16,1,1024]{2,1,0:T(1,128)}, bf16[16,1024,512]{2,1,0:T(8,128)(2,1)}, bf16[2,2008,512]{2,1,0:T(8,128)(2,1)}, s32[16,1,1024]{2,1,0:T(1,128)}) custom-call(bf16[4,1024,512]{2,1,0:T(8,128)(2,1)} %bitcast.7, bf16[4016,512]{1,0:T(8,128)(2,1)} %w.3, s32[4,1,1024]{2,1,0:T(1,128)} %reshape.19.tg), custom_call_target="tpu_custom_call" | custom-call | tf_op jit(solution)/shard_map/fwd/pallas_call | solution.py:491
  187.2 325.9 %bwd.1 = (f32[2,2008,512]{2,1,0:T(8,128)}, f32[2,2008,512]{2,1,0:T(8,128)}, f32[4,512,1024]{2,1,0:T(8,128)}, f32[2,8,128]{2,1,0:T(8,128)}, f32[16,512,1024]{2,1,...) custom-call(bf16[4016,512]{1,0:T(8,128)(2,1)} %w.3, ...), custom_call_target="tpu_custom_call" | custom-call | tf_op jit(solution)/shard_map/bwd/pallas_call | solution.py:508
  513.2 1.3 reduce_sum.9
  514.5 8.7 %copy.6 = f32[4,1024,512]{2,1,0:T(8,128)} copy(f32[4,1024,512]{1,2,0:T(8,128)} %bitcast.4) | data formatting | bytes 16777216 | tf_op jit(solution)/shard_map/transpose | solution.py:527
  523.1 11.1 %add.3 = f32[2,2008,512]{2,1,0:T(8,128)} add(f32[2,2008,512]{2,1,0:T(8,128)} %get-tuple-element.19, f32[2,2008,512]{2,1,0:T(8,128)} %get-tuple-element.20) | non-fusion elementwise | flops 2056192 | bytes 24674304 | tf_op jit(solution)/shard_map/add | solution.py:526

commit v3 on v2

--- a/solution.py
+++ b/solution.py
@@ -13,6 +13,7 @@
 LN2 = 0.6931471805599453
 BT = 1024
 RC = 256
+N_PART = 4
 VMEM_LIMIT = 61 << 20
 ANY = pl.BlockSpec(memory_space=pl.ANY)
 VM = pl.BlockSpec(memory_space=pltpu.VMEM)
@@ -76,7 +77,7 @@
     m_ref[...], s_ref[...] = m, s
 
 
-def bwd_unit(z_ref, lse, tgt, inv, wt_ref, h_ref, dw_ref, dh_ref, tl_ref):
+def bwd_unit(z_ref, lse, tgt, inv, w_ref, h_ref, dw_ref, dh_ref, tl_ref):
     rows = z_ref.shape[0]
     h = h_ref[...]
     tj = tgt - lax.broadcasted_iota(I32, (8, BT), 0)
@@ -95,7 +96,7 @@
         dz = dz.astype(BF16)
         d = jnp.dot(dz[:rm], h, preferred_element_type=F32)
         dw_ref[r0:r0 + rc, :] += d[:rc]
-        d = jnp.dot(wt_ref[:, r0:r0 + rk], dz, preferred_element_type=F32)
+        d = lax.dot_general(dz, w_ref[r0:r0 + rk, :], (((0,), (0,)), ((), ())), preferred_element_type=F32)
         acc = d if acc is None else acc + d
     dh_ref[...] += acc
     tl_ref[...] += tl
@@ -150,7 +151,14 @@
     m[...] = jnp.full_like(m, -jnp.inf)
     s[...] = jnp.zeros_like(s)
 
-    n1 = 4 * n_own
+    s2 = 4 * n_own
+    s3 = s2 + 4
+    s4 = s3 + 2 * n_own
+    s5 = s4 + 4 * (n_own - 2)
+    s6 = s5 + 2 * n_own
+    s7 = s6 + 4
+    first2, first3 = s3, s5
+
     def order(u):
         def near(q):
             return lax.rem(q, 2), q // (2 * n_own), lax.rem(q // 2, n_own)
@@ -161,30 +169,24 @@
         def wide(q, h):
             return jnp.full_like(q, h), q // n_own, lax.rem(q, n_own)
 
-        s2, s3 = n1, n1 + 4
-        s4 = s3 + 2 * n_own
-        s5 = s4 + 4 * (n_own - 2)
-        s6 = s5 + 2 * n_own
-        s7 = s6 + 4
         h7, r7, b7 = far(u - s7, 0)
         return pick(u, [(0, near(u)), (s2, far(u - s2, 0)), (s3, wide(u - s3, 2)), (s4, far(u - s4, 1)),
-                        (s5, wide(u - s5, 3)), (s6, far(u - s6, n_own - 1)), (s7, (h7 + 2, r7, b7))]), s3, s5
+                        (s5, wide(u - s5, 3)), (s6, far(u - s6, n_own - 1)), (s7, (h7 + 2, r7, b7))])
 
     n_units = 4 * 4 * n_own
 
-    def store_z(u):
-        (h, r, b), _, _ = order(u)
-        slot = lax.rem(u, 3)
-        return local(zv.at[slot], z.at[h, blk(r, b)], oz.at[slot])
+    parts = [(q, min(rows, q + up(-(-rows // N_PART), 8))) for q in range(0, rows, up(-(-rows // N_PART), 8))]
+
+    def store_z(h, i, slot):
+        for lo, hi in parts:
+            local(zv.at[slot, pl.ds(lo, hi - lo)], z.at[h, i, pl.ds(lo, hi - lo)], oz.at[slot]).start()
 
     def wait_z(slot):
         local(zv.at[slot], z.at[0, 0], oz.at[slot]).wait()
 
-    @pl.loop(0, n_units)
-    def _(u):
+    def body(u, unit):
+        h, r, b, i = unit
         slot = lax.rem(u, 3)
-        (h, r, b), first2, first3 = order(u)
-        i = blk(r, b)
 
         @pl.when(u < 2)
         def _():
@@ -216,7 +218,13 @@
             wait_z(slot)
 
         fwd_unit(wv.at[h], hv.at[i], zv.at[slot], m.at[i], s.at[i])
-        store_z(u).start()
+        nh, nr, nb = order(u + 1)
+        ni = blk(nr, nb)
+        store_z(h, i, slot)
+        return nh, nr, nb, ni
+
+    start = order(jnp.int32(0))
+    lax.fori_loop(0, n_units, body, (*start, blk(start[1], start[2])))
 
     mm = m[...]
     m1 = jnp.max(mm, axis=1, keepdims=True)
@@ -249,12 +257,13 @@
         wait_z(k)
 
 
-def bwd_kernel(n, tokens, n_micro, w, wpeer, hbuf, tall, lse, z, dwo, rxw, dho, loss, part, rxs, txb, rxb, zblk,
-               wv, wt, hv, zv, dwa, dha, rbuf, tla, lmsg, lrx,
+def bwd_kernel(n, tokens, n_micro, w, wpeer, hbuf, tall, lse, z, dwo, dho, loss, rxw, part, rxs, txb, rxb, zblk,
+               wv, hv, zv, dwa, dha, rbuf, tla, lmsg, lrx,
                lw, lz, lh, li, lr, eo, es, rss, sb, rb, swr, rwr, sl, rl):
     at = Place(n)
     n_own = dho.shape[0]
-    rows, cols = zv.shape[1], wt.shape[2]
+    rows, cols = zv.shape[1], wv.shape[1]
+    dim = wv.shape[2]
     inv = 1.0 / tokens
 
     sem = pltpu.get_barrier_semaphore()
@@ -269,33 +278,41 @@
     v_d = v_c + far - 2
     v_e = v_d + 2 + 2 * n_own
     v_f = v_e + 2
-    n_visits = v_f + 2 * n_own
     u_b = 8
     u_c = u_b + far + 2 * n_own
     u_d = u_c + 3 * (far - 2)
     u_e = u_d + 2 + 2 * n_own
     u_f = u_e + 4
     n_units = u_f + 4 * n_own
-
-    def visit(v):
+    n_visits = v_f + 2 * n_own
+
+    def order(u):
         def far_pair(q, b0):
             return 3 - lax.rem(q, 2), b0 + q // 2
 
         def near_pair(q):
             return 1 - lax.rem(q, 2), q // 2
 
-        one = jnp.ones_like(v)
+        one = jnp.ones_like(u)
         zero = one - 1
-        qb, qc, qd, qe, qf = v - v_b, v - v_c, v - v_d, v - v_e, v - v_f
-        return pick(v, [
-            (0, (4 * one, *far_pair(v, 0), zero, 4 * v, one, one)),
-            (v_b, (one, *far_pair(qb, 1), 2 * one, u_b + qb, one, zero)),
-            (v_b + far, (one, *near_pair(qb - far), 2 * one, u_b + qb, one, zero)),
-            (v_c, (3 * one, *far_pair(qc, 1), 3 * one, u_c + 3 * qc, zero, one)),
-            (v_d, (one, *far_pair(qd, n_own - 1), 3 * one, u_d + qd, zero, zero)),
-            (v_d + 2, (one, *near_pair(qd - 2), 3 * one, u_d + qd, zero, zero)),
-            (v_e, (2 * one, *far_pair(qe, n_own - 1), zero, u_e + 2 * qe, zero, one)),
-            (v_f, (2 * one, *near_pair(qf), zero, u_f + 2 * qf, zero, one)),
+
+        def run(q, count, h0, pair, v0, fresh):
+            k, wv_ = lax.rem(q, count), lax.div(q, jnp.int32(count))
+            return (lax.rem(k + h0, 4), *pair(wv_), (k == 0).astype(I32), (k == count - 1).astype(I32), v0 + wv_, fresh, one)
+
+        def sweep(q, h, pair, v0, fresh):
+            return (h * one, *pair, one, one, v0 + q, fresh, zero)
+
+        qb, qd = u - u_b, u - u_d
+        return pick(u, [
+            (0, run(u, 4, 0, lambda q: far_pair(q, 0), 0, one)),
+            (u_b, sweep(qb, 2, far_pair(qb, 1), v_b, one)),
+            (u_b + far, sweep(qb, 2, near_pair(qb - far), v_b, one)),
+            (u_c, run(u - u_c, 3, 3, lambda q: far_pair(q, 1), v_c, zero)),
+            (u_d, sweep(qd, 3, far_pair(qd, n_own - 1), v_d, zero)),
+            (u_d + 2, sweep(qd, 3, near_pair(qd - 2), v_d, zero)),
+            (u_e, run(u - u_e, 2, 0, lambda q: far_pair(q, n_own - 1), v_e, zero)),
+            (u_f, run(u - u_f, 2, 0, near_pair, v_f, zero)),
         ])
 
     def load_z(h, i, slot):
@@ -304,15 +321,6 @@
     def load_h(i, slot):
         return local(hbuf.at[i], hv.at[slot], lh.at[slot])
 
-    def start_init(i, fresh, slot):
-        @pl.when(fresh == 1)
-        def _():
-            local(zblk, dha.at[slot], li.at[slot]).start()
-
-        @pl.when(fresh == 0)
-        def _():
-            local(part.at[i], dha.at[slot], li.at[slot]).start()
-
     def to_sib(r, b, slot):
         return remote(dha.at[slot], rxs.at[n_own * (1 - r // 2) + b], es.at[slot], rss.at[n_own * (1 - r // 2) + b], at.sib)
 
@@ -325,29 +333,31 @@
     def to_peer(k):
         return remote(dwa.at[2 + k], rxw.at[k], swr.at[k], rwr.at[k], at.peer)
 
+    def load_rx(k):
+        return local(rxw.at[k], zv.at[0, :, pl.ds(k * dim, dim)], lr.at[2 + k])
+
+    halves = [w.at[pl.ds(0, rows)], w.at[pl.ds(rows, rows)], wpeer.at[0], wpeer.at[1]]
+
+    def load_w(k):
+        return local(halves[k], wv.at[k, pl.ds(0, rows)], lw.at[k])
+
+    load_w(0).start()
     load_z(0, blk(3, 0), 0).start()
     load_h(blk(3, 0), 0).start()
+    for k in range(1, 4):
+        load_w(k).start()
     rbuf[0] = jnp.zeros(rbuf.shape[1:], F32)
     local(rbuf.at[0], zblk, lr.at[0]).start()
-    halves = [w.at[pl.ds(0, rows)], w.at[pl.ds(rows, rows)], wpeer.at[0], wpeer.at[1]]
-    local(halves[0], wv.at[0], lw.at[0]).start()
+    if cols > rows:
+        for k in range(4):
+            wv[k, rows:] = jnp.zeros((cols - rows, dim), BF16)
+    dha[0] = jnp.zeros(dha.shape[1:], F32)
     dwa[...] = jnp.zeros_like(dwa)
     tla[...] = jnp.zeros_like(tla)
-    for k in range(4):
-        local(halves[k], wv.at[k % 2], lw.at[k % 2]).wait()
-        if k < 3:
-            local(halves[k + 1], wv.at[(k + 1) % 2], lw.at[(k + 1) % 2]).start()
-        for r0, rc in chunks(rows):
-            wt[k, :, r0:r0 + rc] = wv[k % 2, r0:r0 + rc, :].T
-        if cols > rows:
-            wt[k, :, rows:] = jnp.zeros((wt.shape[1], cols - rows), BF16)
     local(rbuf.at[0], zblk, lr.at[0]).wait()
-    local(zblk, dha.at[0], li.at[0]).start()
     pl.semaphore_wait(sem, n - 1)
 
-    def finish(v):
-        slot = lax.rem(v, 3)
-        _, r, b, _, _, _, comp = visit(v)
+    def finish(r, b, comp, slot):
         sent = jnp.logical_and(comp == 1, lax.rem(r, 2) == 1)
 
         @pl.when(sent)
@@ -362,83 +372,117 @@
         def _():
             to_par(b).start()
 
-    @pl.loop(0, n_visits)
-    def _(v):
-        count, r, b, h0, u0, _, comp = visit(v)
-        _, r_n, b_n, h0_n, _, fresh_n, _ = visit(v + 1)
-        i, i_n = blk(r, b), blk(r_n, b_n)
-        hs, ds = lax.rem(v, 2), lax.rem(v, 3)
-        mine = jnp.logical_and(comp == 1, lax.rem(r, 2) == 0)
+    def body(u, carry):
+        unit, i, nxt, i_n, p1, p2 = carry
+        h, r, b, opens, closes, v, _, comp = unit
+        h_n, fresh_n = nxt[0], nxt[6]
+        slot, hs, ds, ds_n = lax.rem(u, 2), lax.rem(v, 2), lax.rem(v, 3), lax.rem(v + 1, 3)
+        more = u + 1 < n_units
+        odd = lax.rem(r, 2) == 1
+        ends = jnp.logical_and(closes == 1, comp == 1)
+        mine = jnp.logical_and(ends, jnp.logical_not(odd))
         last = jnp.logical_and(mine, r == 0)
 
-        @pl.when(v >= 2)
-        def _():
-            finish(v - 2)
-
-        local(zblk, dha.at[ds], li.at[ds]).wait()
-        load_h(i, hs).wait()
-
-        @pl.when(v + 1 < n_visits)
-        def _():
-            start_init(i_n, fresh_n, lax.rem(v + 1, 3))
-            load_h(i_n, 1 - hs).start()
-
-        @pl.loop(0, count)
-        def _(k):
-            u = u0 + k
-            slot = lax.rem(u, 2)
-            h = lax.rem(h0 + k, 4)
-            end = k + 1 == count
-            load_z(h, i, slot).wait()
-
-            @pl.when(u + 1 < n_units)
-            def _():
-                load_z(jnp.where(end, h0_n, lax.rem(h + 1, 4)), jnp.where(end, i_n, i), 1 - slot).start()
-
-            @pl.when(jnp.logical_and(end, mine))
+        @pl.when(u < 4)
+        def _():
+            local(halves[0], wv.at[h, pl.ds(0, rows)], lw.at[h]).wait()
+
+        load_z(h, i, slot).wait()
+
+        @pl.when(more)
+        def _():
+            load_z(h_n, i_n, 1 - slot).start()
+
+        @pl.when(opens == 1)
+        def _():
+            @pl.when(v >= 2)
+            def _():
+                finish(*p2, ds_n)
+
+            load_h(i, hs).wait()
+
+            @pl.when(v > 0)
+            def _():
+                local(zblk, dha.at[ds], li.at[ds]).wait()
+
+        @pl.when(closes == 1)
+        def _():
+            @pl.when(more)
+            def _():
+                load_h(i_n, 1 - hs).start()
+
+                @pl.when(fresh_n == 1)
+                def _():
+                    local(zblk, dha.at[ds_n], li.at[ds_n]).start()
+
+                @pl.when(fresh_n == 0)
+                def _():
+                    local(part.at[i_n], dha.at[ds_n], li.at[ds_n]).start()
+
+            @pl.when(jnp.logical_not(more))
+            def _():
+                for k in range(2):
+                    to_peer(k).wait_recv()
+                    load_rx(k).start()
+
+            @pl.when(mine)
             def _():
                 from_sib(r, b).wait_recv()
                 local(rxs.at[n_own * (1 - r // 2) + b], rbuf.at[0], lr.at[0]).start()
 
-            @pl.when(jnp.logical_and(end, last))
+            @pl.when(last)
             def _():
                 to_par(b).wait_recv()
                 local(rxb.at[b], rbuf.at[1], lr.at[1]).start()
 
-            base = jnp.where(h < 2, at.me, at.peer) * (2 * rows) + lax.rem(h, 2) * rows
-            bwd_unit(zv.at[slot], lse[i], tall[i] - base, inv, wt.at[h], hv.at[hs], dwa.at[h], dha.at[ds],
-                     tla.at[b // (n_own // n_micro)])
-
-        @pl.when(mine)
-        def _():
-            local(rxs.at[0], rbuf.at[0], lr.at[0]).wait()
-            dha[ds] += rbuf[0]
-
-        @pl.when(last)
-        def _():
-            local(rxb.at[0], rbuf.at[1], lr.at[1]).wait()
-            dha[ds] += rbuf[1]
-            local(dha.at[ds], dho.at[b], eo.at[ds]).start()
-
-        @pl.when(jnp.logical_and(mine, r == 2))
-        def _():
-            local(dha.at[ds], txb.at[b], eo.at[ds]).start()
-
-        @pl.when(jnp.logical_and(comp == 1, lax.rem(r, 2) == 1))
-        def _():
-            to_sib(r, b, ds).start()
-
-        @pl.when(comp == 0)
-        def _():
-            local(dha.at[ds], part.at[i], eo.at[ds]).start()
-
-        @pl.when(v == v_c - 1)
-        def _():
-            to_peer(0).start()
-
-        @pl.when(v == v_e - 1)
-        def _():
-            to_peer(1).start()
+        base = jnp.where(h < 2, at.me, at.peer) * (2 * rows) + lax.rem(h, 2) * rows
+        bwd_unit(zv.at[slot], lse[i], tall[i] - base, inv, wv.at[h], hv.at[hs], dwa.at[h], dha.at[ds],
+                 tla.at[b // (n_own // n_micro)])
+        after = order(u + 2)
+        i_after = blk(after[1], after[2])
+        shift = closes == 1
+        q2 = tuple(jnp.where(shift, x, y) for x, y in zip(p1, p2))
+        q1 = tuple(jnp.where(shift, x, y) for x, y in zip((r, b, comp), p1))
+
+        @pl.when(closes == 1)
+        def _():
+            @pl.when(mine)
+            def _():
+                local(rxs.at[0], rbuf.at[0], lr.at[0]).wait()
+
+                @pl.when(r == 0)
+                def _():
+                    local(rxb.at[0], rbuf.at[1], lr.at[1]).wait()
+                    dha[ds] += rbuf[0] + rbuf[1]
+                    local(dha.at[ds], dho.at[b], eo.at[ds]).start()
+
+                @pl.when(r == 2)
+                def _():
+                    dha[ds] += rbuf[0]
+                    local(dha.at[ds], txb.at[b], eo.at[ds]).start()
+
+            @pl.when(jnp.logical_and(ends, odd))
+            def _():
+                to_sib(r, b, ds).start()
+
+            @pl.when(comp == 0)
+            def _():
+                local(dha.at[ds], part.at[i], eo.at[ds]).start()
+
+                @pl.when(u == u_c - 1)
+                def _():
+                    to_peer(0).start()
+
+                @pl.when(u == u_e - 1)
+                def _():
+                    to_peer(1).start()
+
+        return nxt, i_n, after, i_after, q1, q2
+
+    first, second = order(jnp.int32(0)), order(jnp.int32(1))
+    none = (jnp.int32(0),) * 3
+    _, _, _, _, p1, p2 = lax.fori_loop(
+        0, n_units, body, (first, blk(first[1], first[2]), second, blk(second[1], second[2]), none, none))
 
     per = n_own // n_micro
     top = lax.broadcasted_iota(I32, (8, BT), 0) == 0
@@ -457,10 +501,19 @@
 
     for d in range(1, n):
         send_loss(d).start()
-    own_dw = local(dwa.at[pl.ds(0, 2)], dwo, lw.at[0])
-    own_dw.start()
-    finish(jnp.int32(n_visits - 2))
-    finish(jnp.int32(n_visits - 1))
+    edges = [rows * q // 32 * 8 for q in range(4)] + [rows]
+    pieces = list(zip(edges[:-1], edges[1:]))
+
+    def out_dw(k):
+        return local(dwa.at[k], dwo.at[k], lw.at[k])
+
+    for k in range(2):
+        load_rx(k).wait()
+        for lo, hi in pieces:
+            dwa[k, lo:hi] += zv[0, lo:hi, k * dim:(k + 1) * dim]
+            local(dwa.at[k, pl.ds(lo, hi - lo)], dwo.at[k, pl.ds(lo, hi - lo)], lw.at[k]).start()
+    finish(*p2, lax.rem(jnp.int32(n_visits - 2), 3))
+    finish(*p1, lax.rem(jnp.int32(n_visits - 1), 3))
     for d in range(1, n):
         send_loss(d).wait()
     tot = lmsg[...]
@@ -468,10 +521,11 @@
         tot = tot + lrx[d]
     loss[...] = tot
     for k in range(2):
-        to_peer(k).wait()
+        to_peer(k).wait_send()
     for b in range(n_own):
         to_par(b).wait_send()
-    own_dw.wait()
+    for k in range(2):
+        out_dw(k).wait()
 
 
 def solution(mesh):
@@ -504,27 +558,27 @@
             name='fwd',
         )(hidden.reshape(n_own, BT, dim), w_loc, targets.reshape(n_own, 1, BT))
 
-        blk_shape = (dim, BT)
-        dwo, rxw, dho, loss, *_ = pl.pallas_call(
+        blk_shape = (BT, dim)
+        dwo, dho, loss, *_ = pl.pallas_call(
             functools.partial(bwd_kernel, n, tokens, n_micro),
-            out_shape=(out((2, rows, dim)), out((2, rows, dim)), out((n_own, *blk_shape)), out((n_micro, 8, 128)),
+            out_shape=(out((2, rows, dim)), out((n_own, *blk_shape)), out((n_micro, 8, 128)), out((2, rows, dim)),
                        out((n_blk, *blk_shape)), out((2 * n_own, *blk_shape)), out((n_own, *blk_shape)), out((n_own, *blk_shape)),
                        out(blk_shape)),
             in_specs=[ANY, ANY, ANY, VM, VM, ANY],
-            out_specs=(ANY, ANY, ANY, VM, ANY, ANY, ANY, ANY, ANY),
+            out_specs=(ANY, ANY, VM, ANY, ANY, ANY, ANY, ANY, ANY),
             scratch_shapes=[
-                pltpu.VMEM((2, rows, dim), BF16), pltpu.VMEM((4, dim, up(rows, 256)), BF16), pltpu.VMEM((2, BT, dim), BF16),
+                pltpu.VMEM((4, up(rows, 256), dim), BF16), pltpu.VMEM((2, BT, dim), BF16),
                 pltpu.VMEM((2, rows, BT), F32), pltpu.VMEM((4, rows, dim), F32), pltpu.VMEM((3, *blk_shape), F32),
-                pltpu.VMEM((2, *blk_shape), F32), pltpu.VMEM((n_micro, 8, BT), F32), pltpu.VMEM((n_micro, 8, 128), F32),
-                pltpu.VMEM((n - 1, n_micro, 8, 128), F32),
-                DMA((2,)), DMA((2,)), DMA((2,)), DMA((3,)), DMA((2,)), DMA((3,)), DMA((3,)), DMA((2 * n_own,)),
+                pltpu.VMEM((2, *blk_shape), F32), pltpu.VMEM((n_micro, 8, BT), F32),
+                pltpu.VMEM((n_micro, 8, 128), F32), pltpu.VMEM((n - 1, n_micro, 8, 128), F32),
+                DMA((4,)), DMA((2,)), DMA((2,)), DMA((3,)), DMA((4,)), DMA((3,)), DMA((3,)), DMA((2 * n_own,)),
                 DMA((n_own,)), DMA((n_own,)), DMA((2,)), DMA((2,)), DMA((n - 1,)), DMA((n - 1,))],
             compiler_params=pltpu.CompilerParams(vmem_limit_bytes=VMEM_LIMIT, collective_id=1, has_side_effects=True),
             name='bwd',
         )(w_loc, wpeer, hbuf, tall, lse, z)
 
-        d_w = (dwo + rxw).reshape(vb, dim)
-        d_h = dho.transpose(0, 2, 1).reshape(n_micro, tok_dev, dim)
+        d_w = dwo.reshape(vb, dim)
+        d_h = dho.reshape(n_micro, tok_dev, dim)
         return jnp.sum(loss, axis=(1, 2)), d_h, d_w
 
     return jax.shard_map(local_head, mesh=mesh,

time: 535 us -> 520 us (0.972)
  other arithmetic: 12.4 us -> 1.3 us
  Pallas kernels: 511 us -> 505 us
    unnamed x0 -> x4, local copies, waits for them, and re-layouts: none -> 11.3 us
    add x1 -> x0, other arithmetic: 11.1 us -> none  [local_head(): d_w = (dwo + rxw).reshape(vb, dim)]
    transpose x1 -> x0, local copies, waits for them, and re-layouts: 8.67 us -> none  [local_head(): d_h = dho.transpose(0, 2, 1).reshape(n_micro, tok_dev, dim)]
where the time goes in v3:
time: 520 us; the launch traced here: 519 us
  Pallas kernels  505 us (97%)
  local copies, waits for them, and re-layouts  12.7 us (2%)
    pallas_call x1, Pallas kernels, local_head(): pl.pallas_call(functools.partial(bwd_kernel, n, tokens, n_micro), out_sha...  324 us
    pallas_call x1, Pallas kernels, local_head(): pl.pallas_call(functools.partial(fwd_kernel, n, tokens), out_shape=(out((...  181 us
    unnamed x4, local copies, waits for them, and re-layouts  11.3 us

profile of v3, /device:TPU:113, one launch (start us, length us, event | category | flops | bytes accessed | tf_op | source)
XLA Modules:
  0.0 519.4 jit_solution(9453826122617011105)
XLA Ops:
  0.6 1.4 reshape.19.tg
  2.0 180.5 %fwd.1 = (f32[4,16,2008,1024]{3,2,1,0:T(8,128)}, f32[16,1,1024]{2,1,0:T(1,128)}, bf16[16,1024,512]{2,1,0:T(8,128)(2,1)}, bf16[2,2008,512]{2,1,0:T(8,128)(2,1)}, s32[16,1,1024]{2,1,0:T(1,128)}) custom-call(bf16[4,1024,512]{2,1,0:T(8,128)(2,1)} %bitcast.5, bf16[4016,512]{1,0:T(8,128)(2,1)} %w.3, s32[4,1,1024]{2,1,0:T(1,128)} %reshape.19.tg), custom_call_target="tpu_custom_call" | custom-call | tf_op jit(solution)/shard_map/fwd/pallas_call | solution.py:545
  182.5 324.3 %bwd.1 = (f32[2,2008,512]{2,1,0:T(8,128)}, f32[4,1024,512]{2,1,0:T(8,128)}, f32[2,8,128]{2,1,0:T(8,128)}, f32[2,2008,512]{2,1,0:T(8,128)}, f32[16,1024,512]{2,1,...) custom-call(bf16[4016,512]{1,0:T(8,128)(2,1)} %w.3, ...), custom_call_target="tpu_custom_call" | custom-call | tf_op jit(solution)/shard_map/bwd/pallas_call | solution.py:562
  506.8 1.3 reduce_sum.9
  508.1 0.0 copy-start
  508.1 8.0 %copy.8 = f32[2,2048,512]{2,1,0:T(8,128)} copy(f32[2,2048,512]{2,1,0:T(8,128)} %bitcast.3) | data formatting | bytes 16777216
  516.1 0.0 copy-done
  516.1 3.3 copy.9
Async XLA Ops:
  508.1 8.0 %copy-start = (f32[2,2008,512]{2,1,0:T(8,128)S(1)}, f32[2,2008,512]{2,1,0:T(8,128)}, u32[]{:S(2)}) copy-start(f32[2,2008,512]{2,1,0:T(8,128)} %get-tuple-element.18) | copy-start | bytes 24674308
